TPU v7x, 32 devices: a whole 2x2x4 slice. The times are simulated.
32 devices in a mesh: mkt: 8 (over y, x, core), trade: 1, scen: 4 (over z).
Axes of the slice: x: 2, y: 2, z: 4, core: 2. Of those that a mesh axis runs over, the one named last changes fastest.
Arguments:
- quotes: bfloat16 [512, 512], P('mkt'), may hold values from -6 to 6
- kernel: bfloat16 [64, 128, 128], P(('trade', 'scen')), may hold values from -0.5 to 0.5
- trade_block: int32 [2048], P('trade'), may hold values from 0 to 63
- trade_embed: bfloat16 [2048, 256], P('trade'), may hold values from -6 to 6
- position: float32 [2048], P('trade'), may hold values from -0.125 to 0.125
- scen_rank: int32 [512], P(('mkt', 'scen')), may hold values from 0 to 511, each once
- w_in: bfloat16 [128, 256], replicated, may hold values from -0.5 to 0.5
- w_mid: bfloat16 [256, 256], replicated, may hold values from -0.375 to 0.375
- b_mid: float32 [256], replicated, may hold values from -6 to 6
- w_out: bfloat16 [256], replicated, may hold values from -0.375 to 0.375
Outputs:
- book_pnl: float32 [512], P(('mkt', 'scen'))
- marginal: float32 [2048], P('trade')
- shortfall: float32 [], replicated
Inputs may be any that keep to these rules, and one draw needn't show every extreme that they name: scen_rank holds each rank of 0 to 511 once.
All inputs are finite; a program needn't handle non-finite values.
Results may differ from a plain program's by a relative error of at most 0.014.
The roundings to bfloat16 on the way count: a program that leaves them out, or rounds other values in their place, can miss the bound.
Values may be sent and summed in bfloat16 or wider, within the bound.
No kernel may reach another device: no remote copies, remote signals or barrier semaphores. Data moves between devices by JAX's collectives and lax.ppermute only.
A program may use at most 64 MiB of HBM per device.

v0:
```python
import jax
import jax.numpy as jnp
from jax import lax
from jax.sharding import PartitionSpec as P

SEG = 128
WIN = 128
QSTEP = 8


def local(quotes, kernel, trade_block, trade_embed, position, scen_rank, w_in, w_mid, b_mid, w_out):
    local_count = kernel.shape[0]
    quote_count = quotes.shape[1]
    row_count = quotes.shape[0]
    first_block = lax.axis_index(("trade", "scen")) * local_count

    def cut_window(local_block):
        block_index = first_block + local_block
        window_start = jnp.clip(QSTEP * block_index - (WIN - QSTEP) // 2, 0, quote_count - WIN)
        return lax.dynamic_slice_in_dim(quotes, window_start, WIN, 1)

    windows = jax.vmap(cut_window)(jnp.arange(local_count, dtype=jnp.int32))
    built_state = jnp.einsum("jrw,jws->jrs", windows, kernel, preferred_element_type=jnp.float32)
    built_state = built_state.astype(jnp.bfloat16).reshape(local_count, row_count * SEG)
    scen_count = scen_rank.shape[0]
    quarter = lax.all_to_all(built_state, "scen", split_axis=1, concat_axis=0, tiled=True)
    table = lax.all_gather(quarter, "trade", axis=0, tiled=True)
    trade_rows_all = table[trade_block]
    embed_float = trade_embed.astype(jnp.float32)

    def price(scen_index):
        trade_rows = lax.dynamic_slice_in_dim(trade_rows_all, scen_index * SEG, SEG, 1)
        hidden_one = jax.nn.silu(
            jnp.dot(trade_rows, w_in, preferred_element_type=jnp.float32) + embed_float
        ).astype(jnp.bfloat16)
        hidden_two = jax.nn.silu(
            jnp.dot(hidden_one, w_mid, preferred_element_type=jnp.float32) + b_mid
        ).astype(jnp.bfloat16)
        return jnp.dot(hidden_two, w_out, preferred_element_type=jnp.float32)

    values = lax.map(price, jnp.arange(scen_count, dtype=jnp.int32))
    scen_total = scen_count * lax.axis_size("mkt") * lax.axis_size("scen")
    decay_span = scen_total // 20
    weight_sum = jnp.sum(jnp.exp(-jnp.arange(scen_total, dtype=jnp.float32) / decay_span))
    weights = jnp.exp(-scen_rank.astype(jnp.float32) / decay_span) / weight_sum
    pnl_part = jnp.dot(values, position, precision=lax.Precision.HIGHEST)
    marginal = lax.psum(-jnp.dot(weights, values, precision=lax.Precision.HIGHEST), ("mkt", "scen"))
    book_pnl = lax.psum(pnl_part, "trade")
    local_tail = -jnp.dot(weights, book_pnl, precision=lax.Precision.HIGHEST)
    shortfall = lax.psum(local_tail, ("mkt", "scen"))
    return (book_pnl, marginal, shortfall)


def solution(mesh):
    placed = (
        P("mkt", None),
        P(("trade", "scen"), None, None),
        P("trade"),
        P("trade", None),
        P("trade"),
        P(("mkt", "scen")),
        P(),
        P(),
        P(),
        P(),
    )
    return jax.shard_map(
        local,
        mesh=mesh,
        in_specs=placed,
        out_specs=(P(("mkt", "scen")), P("trade"), P()),
        check_vma=False,
    )
```

profile of v0, /device:TPU:0, one launch (start us, length us, event | category | flops | bytes accessed | tf_op | source)
XLA Modules:
  0.0 204.2 jit_solution(12396054698393962323)
XLA Ops:
  0.7 33.3 %while.12 = (s32[]{:T(128)}, bf16[64,512]{1,0:T(8,128)(2,1)}, s32[16,2]{0,1:T(2,128)S(1)}, bf16[16,64,128]{2,1,0:T(8,128)(2,1)S(1)}, s32[]{:T(128)}) while((s32[]{:T(128)}, bf16[64,512]{1,0:T(8,128)(2,1)}, s32[16,2]{0,1:T(2,128)S(1)}, bf16[16,64,128]{2,1,0:T(8,128)(2,1)S(1)}, s32[]{:T(128)}) %tuple.34), condition=%wide.while_cond, body=%wide.while_body.sunk | while | flops 2 | bytes 32865 | solution.py:20
  35.2 6.0 %all-to-all-start = ((bf16[16,4,2048]{2,0,1:T(8,128)(2,1)}), bf16[16,4,2048]{2,0,1:T(8,128)(2,1)S(1)}, u32[]{:S(2)}, u32[]{:S(2)}) async-start(bf16[16,4,2048]{2,0,1:T(8,128)(2,1)} %copy.14), calls=%async_computation | async-start | bytes 524288 | tf_op jit(solution)/shard_map/all_to_all | solution.py:26
  43.2 6.9 %all-to-all-done = bf16[16,4,2048]{2,0,1:T(8,128)(2,1)S(1)} async-done(((bf16[16,4,2048]{2,0,1:T(8,128)(2,1)}), bf16[16,4,2048]{2,0,1:T(8,128)(2,1)S(1)}, u32[]{:S(2)}, u32[]{:S(2)}) %all-to-all-start) | async-done | bytes 262176 | tf_op jit(solution)/shard_map/all_to_all | solution.py:26
  50.2 11.0 %gather_fusion = bf16[2048,2048]{1,0:T(8,128)(2,1)} fusion(bf16[64,2048]{1,0:T(8,128)(2,1)S(1)} %bitcast.38, s32[2048]{0:T(1024)S(1)} %fusion.6), kind=kCustom, calls=%fused_computation | custom fusion | bytes 16785408 | tf_op jit(solution)/shard_map/gather | solution.py:28
  61.2 100.5 %while.11 = (s32[]{:T(128)}, f32[16,2048]{1,0:T(8,128)S(1)}, s32[16]{0:T(128)S(1)}, bf16[2048,2048]{1,0:T(8,128)(2,1)}, bf16[128,256]{1,0:T(8,128)(2,1)S(1)}, /*...) while((s32[]{:T(128)}, f32[16,2048]{1,0:T(8,128)S(1)}, ...), condition=%wide.region_1.2_spmd, body=%wide.region_0.1_spmd.sunk | while | flops 409993216 | bytes 4942527 | solution.py:41
  62.4 2.8 %multiply_convert_fusion.3 = bf16[2048,256]{1,0:T(8,128)(2,1)} fusion(f32[2048,256]{1,0:T(8,128)S(1)} %get-tuple-element.215, bf16[128,256]{1,0:T(8,128)(2,1)S(1)} %get-tuple-element.214, bf16[2048,2048]{1,0:T(8,128)(2,1)} %get-tuple-element.213, s32[]{:T(128)S(6)} %select_n.23), kind=kOutput, calls=%fused_computation.4.clone.1 | convolution fusion | flops 137363456 | bytes 3735556 | tf_op jit(solution)/shard_map/while/body/eval_jaxpr/dot_general | solution.py:34
  65.2 2.0 %fusion.29 = f32[1,2048]{1,0:T(1,128)S(1)} fusion(bf16[256,1]{0,1:T(2,128)(2,1)S(1)} %reshape.77, bf16[2048,256]{1,0:T(8,128)(2,1)} %multiply_convert_fusion.3, bf16[256,256]{1,0:T(8,128)(2,1)S(1)} %get-tuple-element.216, f32[256]{0:T(256)S(1)} %get-tuple-element.217), kind=kOutput, calls=%fused_computation.5.clone.1 | convolution fusion | flops 272629760 | bytes 1189376 | tf_op jit(solution)/shard_map/while/body/eval_jaxpr/dot_general | solution.py:39
  68.7 2.8 %multiply_convert_fusion.3 = bf16[2048,256]{1,0:T(8,128)(2,1)} fusion(f32[2048,256]{1,0:T(8,128)S(1)} %get-tuple-element.215, bf16[128,256]{1,0:T(8,128)(2,1)S(1)} %get-tuple-element.214, bf16[2048,2048]{1,0:T(8,128)(2,1)} %get-tuple-element.213, s32[]{:T(128)S(6)} %select_n.23), kind=kOutput, calls=%fused_computation.4.clone.1 | convolution fusion | flops 137363456 | bytes 3735556 | tf_op jit(solution)/shard_map/while/body/eval_jaxpr/dot_general | solution.py:34
  71.5 2.0 %fusion.29 = f32[1,2048]{1,0:T(1,128)S(1)} fusion(bf16[256,1]{0,1:T(2,128)(2,1)S(1)} %reshape.77, bf16[2048,256]{1,0:T(8,128)(2,1)} %multiply_convert_fusion.3, bf16[256,256]{1,0:T(8,128)(2,1)S(1)} %get-tuple-element.216, f32[256]{0:T(256)S(1)} %get-tuple-element.217), kind=kOutput, calls=%fused_computation.5.clone.1 | convolution fusion | flops 272629760 | bytes 1189376 | tf_op jit(solution)/shard_map/while/body/eval_jaxpr/dot_general | solution.py:39
  75.0 2.8 %multiply_convert_fusion.3 = bf16[2048,256]{1,0:T(8,128)(2,1)} fusion(f32[2048,256]{1,0:T(8,128)S(1)} %get-tuple-element.215, bf16[128,256]{1,0:T(8,128)(2,1)S(1)} %get-tuple-element.214, bf16[2048,2048]{1,0:T(8,128)(2,1)} %get-tuple-element.213, s32[]{:T(128)S(6)} %select_n.23), kind=kOutput, calls=%fused_computation.4.clone.1 | convolution fusion | flops 137363456 | bytes 3735556 | tf_op jit(solution)/shard_map/while/body/eval_jaxpr/dot_general | solution.py:34
  81.3 2.8 %multiply_convert_fusion.3 = bf16[2048,256]{1,0:T(8,128)(2,1)} fusion(f32[2048,256]{1,0:T(8,128)S(1)} %get-tuple-element.215, bf16[128,256]{1,0:T(8,128)(2,1)S(1)} %get-tuple-element.214, bf16[2048,2048]{1,0:T(8,128)(2,1)} %get-tuple-element.213, s32[]{:T(128)S(6)} %select_n.23), kind=kOutput, calls=%fused_computation.4.clone.1 | convolution fusion | flops 137363456 | bytes 3735556 | tf_op jit(solution)/shard_map/while/body/eval_jaxpr/dot_general | solution.py:34
  84.1 2.0 %fusion.29 = f32[1,2048]{1,0:T(1,128)S(1)} fusion(bf16[256,1]{0,1:T(2,128)(2,1)S(1)} %reshape.77, bf16[2048,256]{1,0:T(8,128)(2,1)} %multiply_convert_fusion.3, bf16[256,256]{1,0:T(8,128)(2,1)S(1)} %get-tuple-element.216, f32[256]{0:T(256)S(1)} %get-tuple-element.217), kind=kOutput, calls=%fused_computation.5.clone.1 | convolution fusion | flops 272629760 | bytes 1189376 | tf_op jit(solution)/shard_map/while/body/eval_jaxpr/dot_general | solution.py:39
  87.6 2.8 %multiply_convert_fusion.3 = bf16[2048,256]{1,0:T(8,128)(2,1)} fusion(f32[2048,256]{1,0:T(8,128)S(1)} %get-tuple-element.215, bf16[128,256]{1,0:T(8,128)(2,1)S(1)} %get-tuple-element.214, bf16[2048,2048]{1,0:T(8,128)(2,1)} %get-tuple-element.213, s32[]{:T(128)S(6)} %select_n.23), kind=kOutput, calls=%fused_computation.4.clone.1 | convolution fusion | flops 137363456 | bytes 3735556 | tf_op jit(solution)/shard_map/while/body/eval_jaxpr/dot_general | solution.py:34
  90.4 2.0 %fusion.29 = f32[1,2048]{1,0:T(1,128)S(1)} fusion(bf16[256,1]{0,1:T(2,128)(2,1)S(1)} %reshape.77, bf16[2048,256]{1,0:T(8,128)(2,1)} %multiply_convert_fusion.3, bf16[256,256]{1,0:T(8,128)(2,1)S(1)} %get-tuple-element.216, f32[256]{0:T(256)S(1)} %get-tuple-element.217), kind=kOutput, calls=%fused_computation.5.clone.1 | convolution fusion | flops 272629760 | bytes 1189376 | tf_op jit(solution)/shard_map/while/body/eval_jaxpr/dot_general | solution.py:39
  93.8 2.8 %multiply_convert_fusion.3 = bf16[2048,256]{1,0:T(8,128)(2,1)} fusion(f32[2048,256]{1,0:T(8,128)S(1)} %get-tuple-element.215, bf16[128,256]{1,0:T(8,128)(2,1)S(1)} %get-tuple-element.214, bf16[2048,2048]{1,0:T(8,128)(2,1)} %get-tuple-element.213, s32[]{:T(128)S(6)} %select_n.23), kind=kOutput, calls=%fused_computation.4.clone.1 | convolution fusion | flops 137363456 | bytes 3735556 | tf_op jit(solution)/shard_map/while/body/eval_jaxpr/dot_general | solution.py:34
  100.1 2.8 %multiply_convert_fusion.3 = bf16[2048,256]{1,0:T(8,128)(2,1)} fusion(f32[2048,256]{1,0:T(8,128)S(1)} %get-tuple-element.215, bf16[128,256]{1,0:T(8,128)(2,1)S(1)} %get-tuple-element.214, bf16[2048,2048]{1,0:T(8,128)(2,1)} %get-tuple-element.213, s32[]{:T(128)S(6)} %select_n.23), kind=kOutput, calls=%fused_computation.4.clone.1 | convolution fusion | flops 137363456 | bytes 3735556 | tf_op jit(solution)/shard_map/while/body/eval_jaxpr/dot_general | solution.py:34
  106.4 2.8 %multiply_convert_fusion.3 = bf16[2048,256]{1,0:T(8,128)(2,1)} fusion(f32[2048,256]{1,0:T(8,128)S(1)} %get-tuple-element.215, bf16[128,256]{1,0:T(8,128)(2,1)S(1)} %get-tuple-element.214, bf16[2048,2048]{1,0:T(8,128)(2,1)} %get-tuple-element.213, s32[]{:T(128)S(6)} %select_n.23), kind=kOutput, calls=%fused_computation.4.clone.1 | convolution fusion | flops 137363456 | bytes 3735556 | tf_op jit(solution)/shard_map/while/body/eval_jaxpr/dot_general | solution.py:34
  109.2 2.0 %fusion.29 = f32[1,2048]{1,0:T(1,128)S(1)} fusion(bf16[256,1]{0,1:T(2,128)(2,1)S(1)} %reshape.77, bf16[2048,256]{1,0:T(8,128)(2,1)} %multiply_convert_fusion.3, bf16[256,256]{1,0:T(8,128)(2,1)S(1)} %get-tuple-element.216, f32[256]{0:T(256)S(1)} %get-tuple-element.217), kind=kOutput, calls=%fused_computation.5.clone.1 | convolution fusion | flops 272629760 | bytes 1189376 | tf_op jit(solution)/shard_map/while/body/eval_jaxpr/dot_general | solution.py:39
  112.7 2.8 %multiply_convert_fusion.3 = bf16[2048,256]{1,0:T(8,128)(2,1)} fusion(f32[2048,256]{1,0:T(8,128)S(1)} %get-tuple-element.215, bf16[128,256]{1,0:T(8,128)(2,1)S(1)} %get-tuple-element.214, bf16[2048,2048]{1,0:T(8,128)(2,1)} %get-tuple-element.213, s32[]{:T(128)S(6)} %select_n.23), kind=kOutput, calls=%fused_computation.4.clone.1 | convolution fusion | flops 137363456 | bytes 3735556 | tf_op jit(solution)/shard_map/while/body/eval_jaxpr/dot_general | solution.py:34
  115.5 2.0 %fusion.29 = f32[1,2048]{1,0:T(1,128)S(1)} fusion(bf16[256,1]{0,1:T(2,128)(2,1)S(1)} %reshape.77, bf16[2048,256]{1,0:T(8,128)(2,1)} %multiply_convert_fusion.3, bf16[256,256]{1,0:T(8,128)(2,1)S(1)} %get-tuple-element.216, f32[256]{0:T(256)S(1)} %get-tuple-element.217), kind=kOutput, calls=%fused_computation.5.clone.1 | convolution fusion | flops 272629760 | bytes 1189376 | tf_op jit(solution)/shard_map/while/body/eval_jaxpr/dot_general | solution.py:39
  119.0 2.8 %multiply_convert_fusion.3 = bf16[2048,256]{1,0:T(8,128)(2,1)} fusion(f32[2048,256]{1,0:T(8,128)S(1)} %get-tuple-element.215, bf16[128,256]{1,0:T(8,128)(2,1)S(1)} %get-tuple-element.214, bf16[2048,2048]{1,0:T(8,128)(2,1)} %get-tuple-element.213, s32[]{:T(128)S(6)} %select_n.23), kind=kOutput, calls=%fused_computation.4.clone.1 | convolution fusion | flops 137363456 | bytes 3735556 | tf_op jit(solution)/shard_map/while/body/eval_jaxpr/dot_general | solution.py:34
  125.2 2.8 %multiply_convert_fusion.3 = bf16[2048,256]{1,0:T(8,128)(2,1)} fusion(f32[2048,256]{1,0:T(8,128)S(1)} %get-tuple-element.215, bf16[128,256]{1,0:T(8,128)(2,1)S(1)} %get-tuple-element.214, bf16[2048,2048]{1,0:T(8,128)(2,1)} %get-tuple-element.213, s32[]{:T(128)S(6)} %select_n.23), kind=kOutput, calls=%fused_computation.4.clone.1 | convolution fusion | flops 137363456 | bytes 3735556 | tf_op jit(solution)/shard_map/while/body/eval_jaxpr/dot_general | solution.py:34
  131.5 2.8 %multiply_convert_fusion.3 = bf16[2048,256]{1,0:T(8,128)(2,1)} fusion(f32[2048,256]{1,0:T(8,128)S(1)} %get-tuple-element.215, bf16[128,256]{1,0:T(8,128)(2,1)S(1)} %get-tuple-element.214, bf16[2048,2048]{1,0:T(8,128)(2,1)} %get-tuple-element.213, s32[]{:T(128)S(6)} %select_n.23), kind=kOutput, calls=%fused_computation.4.clone.1 | convolution fusion | flops 137363456 | bytes 3735556 | tf_op jit(solution)/shard_map/while/body/eval_jaxpr/dot_general | solution.py:34
  134.3 2.0 %fusion.29 = f32[1,2048]{1,0:T(1,128)S(1)} fusion(bf16[256,1]{0,1:T(2,128)(2,1)S(1)} %reshape.77, bf16[2048,256]{1,0:T(8,128)(2,1)} %multiply_convert_fusion.3, bf16[256,256]{1,0:T(8,128)(2,1)S(1)} %get-tuple-element.216, f32[256]{0:T(256)S(1)} %get-tuple-element.217), kind=kOutput, calls=%fused_computation.5.clone.1 | convolution fusion | flops 272629760 | bytes 1189376 | tf_op jit(solution)/shard_map/while/body/eval_jaxpr/dot_general | solution.py:39
  137.8 2.8 %multiply_convert_fusion.3 = bf16[2048,256]{1,0:T(8,128)(2,1)} fusion(f32[2048,256]{1,0:T(8,128)S(1)} %get-tuple-element.215, bf16[128,256]{1,0:T(8,128)(2,1)S(1)} %get-tuple-element.214, bf16[2048,2048]{1,0:T(8,128)(2,1)} %get-tuple-element.213, s32[]{:T(128)S(6)} %select_n.23), kind=kOutput, calls=%fused_computation.4.clone.1 | convolution fusion | flops 137363456 | bytes 3735556 | tf_op jit(solution)/shard_map/while/body/eval_jaxpr/dot_general | solution.py:34
  140.6 2.0 %fusion.29 = f32[1,2048]{1,0:T(1,128)S(1)} fusion(bf16[256,1]{0,1:T(2,128)(2,1)S(1)} %reshape.77, bf16[2048,256]{1,0:T(8,128)(2,1)} %multiply_convert_fusion.3, bf16[256,256]{1,0:T(8,128)(2,1)S(1)} %get-tuple-element.216, f32[256]{0:T(256)S(1)} %get-tuple-element.217), kind=kOutput, calls=%fused_computation.5.clone.1 | convolution fusion | flops 272629760 | bytes 1189376 | tf_op jit(solution)/shard_map/while/body/eval_jaxpr/dot_general | solution.py:39
  144.1 2.8 %multiply_convert_fusion.3 = bf16[2048,256]{1,0:T(8,128)(2,1)} fusion(f32[2048,256]{1,0:T(8,128)S(1)} %get-tuple-element.215, bf16[128,256]{1,0:T(8,128)(2,1)S(1)} %get-tuple-element.214, bf16[2048,2048]{1,0:T(8,128)(2,1)} %get-tuple-element.213, s32[]{:T(128)S(6)} %select_n.23), kind=kOutput, calls=%fused_computation.4.clone.1 | convolution fusion | flops 137363456 | bytes 3735556 | tf_op jit(solution)/shard_map/while/body/eval_jaxpr/dot_general | solution.py:34
  150.4 2.8 %multiply_convert_fusion.3 = bf16[2048,256]{1,0:T(8,128)(2,1)} fusion(f32[2048,256]{1,0:T(8,128)S(1)} %get-tuple-element.215, bf16[128,256]{1,0:T(8,128)(2,1)S(1)} %get-tuple-element.214, bf16[2048,2048]{1,0:T(8,128)(2,1)} %get-tuple-element.213, s32[]{:T(128)S(6)} %select_n.23), kind=kOutput, calls=%fused_computation.4.clone.1 | convolution fusion | flops 137363456 | bytes 3735556 | tf_op jit(solution)/shard_map/while/body/eval_jaxpr/dot_general | solution.py:34
  153.2 2.0 %fusion.29 = f32[1,2048]{1,0:T(1,128)S(1)} fusion(bf16[256,1]{0,1:T(2,128)(2,1)S(1)} %reshape.77, bf16[2048,256]{1,0:T(8,128)(2,1)} %multiply_convert_fusion.3, bf16[256,256]{1,0:T(8,128)(2,1)S(1)} %get-tuple-element.216, f32[256]{0:T(256)S(1)} %get-tuple-element.217), kind=kOutput, calls=%fused_computation.5.clone.1 | convolution fusion | flops 272629760 | bytes 1189376 | tf_op jit(solution)/shard_map/while/body/eval_jaxpr/dot_general | solution.py:39
  156.7 2.8 %multiply_convert_fusion.3 = bf16[2048,256]{1,0:T(8,128)(2,1)} fusion(f32[2048,256]{1,0:T(8,128)S(1)} %get-tuple-element.215, bf16[128,256]{1,0:T(8,128)(2,1)S(1)} %get-tuple-element.214, bf16[2048,2048]{1,0:T(8,128)(2,1)} %get-tuple-element.213, s32[]{:T(128)S(6)} %select_n.23), kind=kOutput, calls=%fused_computation.4.clone.1 | convolution fusion | flops 137363456 | bytes 3735556 | tf_op jit(solution)/shard_map/while/body/eval_jaxpr/dot_general | solution.py:34
  159.5 2.0 %fusion.29 = f32[1,2048]{1,0:T(1,128)S(1)} fusion(bf16[256,1]{0,1:T(2,128)(2,1)S(1)} %reshape.77, bf16[2048,256]{1,0:T(8,128)(2,1)} %multiply_convert_fusion.3, bf16[256,256]{1,0:T(8,128)(2,1)S(1)} %get-tuple-element.216, f32[256]{0:T(256)S(1)} %get-tuple-element.217), kind=kOutput, calls=%fused_computation.5.clone.1 | convolution fusion | flops 272629760 | bytes 1189376 | tf_op jit(solution)/shard_map/while/body/eval_jaxpr/dot_general | solution.py:39
  165.3 39.0 %all-reduce.1 = (f32[2048]{0:T(1024)}, f32[]{:T(128)}) all-reduce(f32[2048]{0:T(1024)S(1)} %neg.21, f32[]{:T(128)S(6)} %neg.22), channel_id=1, replica_groups=mesh['mkt'=8,'trade'=1,'scen'=4] {'mkt','scen'}, use_global_device_ids=true, to_apply=%region_3.4 | all-reduce | flops 2049 | bytes 16392 | tf_op jit(solution)/shard_map/psum | solution.py:47
  (132 shorter events, 63.9 us)
Async XLA Ops:
  0.6 33.4 %copy-start = (bf16[16,128,128]{2,1,0:T(8,128)(2,1)S(1)}, bf16[16,128,128]{2,1,0:T(8,128)(2,1)}, u32[]{:S(2)}) copy-start(bf16[16,128,128]{2,1,0:T(8,128)(2,1)} %param.13) | copy-start | bytes 1572868
  34.4 8.9 %copy-start.2 = (s32[2048]{0:T(1024)S(1)}, s32[2048]{0:T(1024)}, u32[]{:S(2)}) copy-start(s32[2048]{0:T(1024)} %param.14) | copy-start | bytes 24580
  35.2 14.9 %all-to-all-start = ((bf16[16,4,2048]{2,0,1:T(8,128)(2,1)}), bf16[16,4,2048]{2,0,1:T(8,128)(2,1)S(1)}, u32[]{:S(2)}, u32[]{:S(2)}) async-start(bf16[16,4,2048]{2,0,1:T(8,128)(2,1)} %copy.14), calls=%async_computation | async-start | bytes 524288 | tf_op jit(solution)/shard_map/all_to_all | solution.py:26
  50.1 11.0 %copy-start.4 = (bf16[256,256]{1,0:T(8,128)(2,1)S(1)}, bf16[256,256]{1,0:T(8,128)(2,1)}, u32[]{:S(2)}) copy-start(bf16[256,256]{1,0:T(8,128)(2,1)} %param.19) | copy-start | bytes 393220
  50.1 11.0 %copy-start.5 = (bf16[128,256]{1,0:T(8,128)(2,1)S(1)}, bf16[128,256]{1,0:T(8,128)(2,1)}, u32[]{:S(2)}) copy-start(bf16[128,256]{1,0:T(8,128)(2,1)} %param.18) | copy-start | bytes 196612
  50.1 11.0 %copy-start.6 = (f32[256]{0:T(256)S(1)}, f32[256]{0:T(256)}, u32[]{:S(2)}) copy-start(f32[256]{0:T(256)} %param.20) | copy-start | bytes 3076
  50.2 11.0 %copy-start.7 = (bf16[256]{0:T(256)(128)(2,1)S(1)}, bf16[256]{0:T(256)(128)(2,1)}, u32[]{:S(2)}) copy-start(bf16[256]{0:T(256)(128)(2,1)} %param.21) | copy-start | bytes 1540
  61.1 100.6 %copy-start.3 = (s32[16]{0:T(128)S(1)}, s32[16]{0:T(128)}, u32[]{:S(2)}) copy-start(s32[16]{0:T(128)} %param.17) | copy-start | bytes 196
  61.2 101.4 %copy-start.1 = (f32[2048]{0:T(1024)S(1)}, f32[2048]{0:T(1024)}, u32[]{:S(2)}) copy-start(f32[2048]{0:T(1024)} %param.16) | copy-start | bytes 24580
where the time goes:
time: 207 us; the launch traced here: 204 us
  matrix products  80.6 us (39%)
  local copies, waits for them, and re-layouts  57.4 us (28%)
  blocking collectives  39 us (19%)
  loops' own time  10.9 us (5%)
  waiting for transfers between devices  6.9 us (3%)
  starting transfers between devices  6.02 us (3%)
    dot_general x16, matrix products, price(): jnp.dot(trade_rows, w_in, preferred_element_type=jnp.float32) + embed_float  44.7 us
    psum x1, blocking collectives, local(): lax.psum(-jnp.dot(weights, values, precision=lax.Precision.HIGHEST), ('mk...  39 us
    gather x48, local copies, waits for them, and re-layouts  33.3 us
    dot_general x16, matrix products, price(): return jnp.dot(hidden_two, w_out, preferred_element_type=jnp.float32)  32.7 us
    gather x1, local copies, waits for them, and re-layouts, local(): trade_rows_all = table[trade_block]  11 us
    another operation x1, loops' own time, local(): values = lax.map(price, jnp.arange(scen_count, dtype=jnp.int32))  10.9 us
    dynamic_slice x16, local copies, waits for them, and re-layouts, local(): values = lax.map(price, jnp.arange(scen_count, dtype=jnp.int32))  9.38 us
    all_to_all x1, waiting for transfers between devices, local(): lax.all_to_all(built_state, 'scen', split_axis=1, concat_axis=0, tiled=True)  6.9 us
  transfers between devices with their start and end apart: 1, of which 1 were waited for; matrix products, arithmetic and copies ran while one was open for 1% of the time, Pallas kernels for 0%

commit v1 on v0

v1 whole, which is shorter than its diff:
```python
import functools

import jax
import jax.numpy as jnp
from jax import lax
from jax.experimental import pallas as pl
from jax.experimental.pallas import tpu as pltpu
from jax.sharding import PartitionSpec as P

QSTEP = 8
LANES = 128
SLOTS = 4
GROUP = 64
STEP = 4
BF = jnp.bfloat16
F32 = jnp.float32
NT = (((1,), (1,)), ((), ()))
HIGH = lax.Precision.HIGHEST


def iota(shape, dim):
    return lax.broadcasted_iota(jnp.int32, shape, dim)


def split3(x):
    high = x.astype(BF)
    rest = x - high.astype(F32)
    mid = rest.astype(BF)
    low = (rest - mid.astype(F32)).astype(BF)
    return high.astype(F32), mid.astype(F32), low.astype(F32)


def build_states(first, quotes_ref, kernel_ref, emit):
    local_count, window, _ = kernel_ref.shape
    quote_count = quotes_ref.shape[1]
    lane = iota((1, window), 1)
    for j in range(local_count):
        start = jnp.clip(QSTEP * (first + j) - (window - QSTEP) // 2, 0, quote_count - window)
        tile = start // window
        back = window - (start - tile * window)
        after = jnp.minimum(tile + 1, quote_count // window - 1)
        low = quotes_ref[:, pl.ds(pl.multiple_of(tile * window, window), window)].astype(F32)
        high = quotes_ref[:, pl.ds(pl.multiple_of(after * window, window), window)].astype(F32)
        cut = jnp.where(lane < back, pltpu.roll(low, back, 1), pltpu.roll(high, back, 1)).astype(BF)
        emit(j, jnp.dot(cut, kernel_ref[j], preferred_element_type=F32).astype(BF))


def states_kernel(first_ref, quotes_ref, kernel_ref, out_ref):
    def emit(j, state):
        out_ref[j] = state

    build_states(first_ref[0], quotes_ref, kernel_ref, emit)


def price_kernel(fused, scen_size, local_count, span, total, *refs):
    block_ref, position_ref, b_mid_ref, w_out_ref, *refs = refs
    rank_refs, refs = refs[:scen_size], refs[scen_size:]
    embed_hbm, w_in_hbm, w_mid_hbm, *refs = refs
    sources, refs = (refs[:2], refs[2:]) if fused else (refs[:1], refs[1:])
    send_ref, embed_ref, w_in_ref, w_mid_ref, *refs = refs
    held, refs = (refs[:2], refs[2:]) if fused else (refs[:1], refs[1:])
    (pre_ref, embed32_ref, meta_ref, hot_ref, place_ref, index_ref, index_smem, listed_ref, value_ref, first_a, first_b,
     second_a, second_b, sum_ref, sems) = refs
    rows = block_ref.shape[0]
    trades = rows * LANES
    block_rows = SLOTS * GROUP
    _, scenarios, hidden = pre_ref.shape
    tile_rows = SLOTS * scenarios
    loads = []
    for n, (source, target) in enumerate(
        zip((*sources, w_in_hbm, embed_hbm, w_mid_hbm), (*held, w_in_ref, embed_ref, w_mid_ref))
    ):
        loads.append(pltpu.make_async_copy(source, target, sems.at[n]))
        loads[-1].start()
    z = lax.axis_index("scen")

    block = block_ref[...]
    group = block // local_count
    mine = group % scen_size == z
    slot = ((group // scen_size) * local_count + block % local_count).astype(F32)
    flag = jnp.where(mine, 1.0, 0.0)
    flag16 = flag.astype(BF)
    upper = jnp.where(iota((LANES, LANES), 0) < iota((LANES, LANES), 1), 1.0, 0.0).astype(BF)
    lower = jnp.where(iota((rows, rows), 0) > iota((rows, rows), 1), 1.0, 0.0).astype(BF)
    inside = jnp.dot(flag16, upper, preferred_element_type=F32)
    above = jnp.sum(jnp.dot(lower, flag16, preferred_element_type=F32), axis=1, keepdims=True)
    place_ref[...] = jnp.where(mine, inside + above, -1.0)
    count = jnp.sum(flag).astype(jnp.int32)
    blocks = pl.cdiv(count, block_rows)

    high, mid, low = split3(position_ref[...])
    line = iota((16, LANES), 0)
    column = iota((16, LANES), 1).astype(F32)
    for r in range(rows):
        one = slice(r, r + 1)
        packed = jnp.where(line == 0, slot[one], jnp.where(line == 1, float(r), column))
        packed = jnp.where(line == 3, high[one], packed)
        packed = jnp.where(line == 4, mid[one], packed)
        packed = jnp.where(line == 5, low[one], packed)
        meta_ref[:, r * LANES : (r + 1) * LANES] = packed.astype(BF)
    index_ref[...] = jnp.zeros_like(index_ref)

    def list_block(b, carry):
        row = iota((block_rows, LANES), 0)
        want = (b * block_rows + SLOTS * (row % GROUP) + row // GROUP).astype(F32)
        for r in range(rows):
            hit = place_ref[r : r + 1, :] == want
            hot_ref[b, :, r * LANES : (r + 1) * LANES] = jnp.where(hit, 1.0, 0.0).astype(BF)
        found = lax.dot_general(meta_ref[...], hot_ref[b], NT, preferred_element_type=F32)
        index = (found[0:1] * rows + found[1:2]) * LANES + found[2:3]
        index_ref[pl.ds(b, 1), :] = index.astype(jnp.int32)
        listed_ref[pl.ds(b, 1), :] = found[3:4] + found[4:5] + found[5:6]
        return carry

    lax.fori_loop(0, blocks, list_block, 0)
    copy = pltpu.make_async_copy(index_ref, index_smem, sems.at[len(loads)])
    copy.start()

    for load in loads[:-2]:
        load.wait()
    w_in = w_in_ref[...] * BF(0.5)

    def emit(j, state):
        pre_ref[j] = jnp.dot(state, w_in, preferred_element_type=F32)

    if fused:
        build_states(z * local_count, *held, emit)
    else:

        def each(j, carry):
            emit(j, held[0][j])
            return carry

        lax.fori_loop(0, held[0].shape[0], each, 0)
    loads[-2].wait()
    embed32_ref[...] = embed_ref[...].astype(F32) * 0.5
    value_ref[...] = jnp.zeros_like(value_ref)
    loads[-1].wait()
    w_mid_ref[...] = w_mid_ref[...] * BF(0.5)
    bias = b_mid_ref[...] * 0.5
    w_out = jnp.broadcast_to(w_out_ref[...], (16, hidden))
    copy.wait()

    def first_stage(step, out_ref):
        for t in range(STEP):
            tile = step * STEP + t
            for k in range(SLOTS):
                entry = index_smem[tile // GROUP, k * GROUP + tile % GROUP]
                half = pre_ref[entry // trades] + embed32_ref[pl.ds(entry % trades, 1), :]
                at = t * tile_rows + k * scenarios
                out_ref[at : at + scenarios, :] = (half * (jnp.tanh(half) + 1.0)).astype(BF)

    def second_stage(in_ref, out_ref):
        for t in range(STEP):
            at = slice(t * tile_rows, (t + 1) * tile_rows)
            half = jnp.dot(in_ref[at, :], w_mid_ref[...], preferred_element_type=F32) + bias
            out_ref[at, :] = (half * (jnp.tanh(half) + 1.0)).astype(BF)

    def third_stage(step, in_ref):
        for t in range(STEP):
            at = slice(t * tile_rows, (t + 1) * tile_rows)
            value = lax.dot_general(w_out, in_ref[at, :], NT, preferred_element_type=F32)
            value_ref[pl.ds(step * STEP + t, 1), :] = value[0:1]

    def price(pair, carry):
        third_stage(2 * pair, second_a)
        second_stage(first_b, second_b)
        first_stage(2 * pair, first_a)
        third_stage(2 * pair + 1, second_b)
        second_stage(first_a, second_a)
        first_stage(2 * pair + 1, first_b)
        return carry

    steps = pl.cdiv(count, SLOTS * STEP)
    lax.fori_loop(0, pl.cdiv(steps + 2, 2), price, 0)

    ranks = jnp.concatenate([ref[...] for ref in rank_refs] * SLOTS, axis=1).astype(F32)
    weight_sum = jnp.sum(jnp.exp(-iota((8, total), 1).astype(F32) / span), axis=1, keepdims=True)[0:1]
    weight = pltpu.roll(jnp.exp(-ranks / span) / weight_sum, z * rank_refs[0].shape[1], 1)
    own = iota((16, tile_rows), 0) == iota((16, tile_rows), 1) // scenarios
    weights = jnp.where(own, jnp.broadcast_to(weight, (16, tile_rows)), 0.0)
    sum_ref[...] = jnp.zeros_like(sum_ref)

    def weigh(b, book):
        value = value_ref[pl.ds(pl.multiple_of(b * GROUP + 2 * STEP, 8), GROUP), :]
        tail = lax.dot_general(weights, value, NT, precision=HIGH, preferred_element_type=F32)
        tail = jnp.concatenate([tail[k : k + 1, :] for k in range(SLOTS)], axis=1)
        stack = jnp.concatenate([*split3(tail), jnp.zeros((13, block_rows), F32)], axis=0).astype(BF)
        sum_ref[...] += jnp.dot(stack, hot_ref[b], preferred_element_type=F32)
        listed = listed_ref[pl.ds(b, 1), :]
        listed = jnp.concatenate(
            [listed[:, k * GROUP : (k + 1) * GROUP] for k in range(SLOTS)] + [jnp.zeros((16 - SLOTS, GROUP), F32)], axis=0
        )
        return book + jnp.dot(listed, value, precision=HIGH, preferred_element_type=F32)

    book = lax.fori_loop(0, blocks, weigh, jnp.zeros((16, tile_rows), F32))
    book = jnp.sum(jnp.where(own, book, 0.0), axis=0, keepdims=True)
    loss = -jnp.sum(book * weight, axis=1, keepdims=True)
    book = sum(book[:, k * scenarios : (k + 1) * scenarios] for k in range(SLOTS))
    tail = -(sum_ref[0:1] + sum_ref[1:2] + sum_ref[2:3])
    rest = jnp.zeros((1, send_ref.shape[2] - trades - scenarios - 1), F32)
    row = jnp.concatenate([tail, book, loss, rest], axis=1)
    for p in range(send_ref.shape[0]):
        send_ref[p] = row


def local(quotes, kernel, trade_block, trade_embed, position, scen_rank, w_in, w_mid, b_mid, w_out):
    trade_size, scen_size, mkt_size = lax.axis_size("trade"), lax.axis_size("scen"), lax.axis_size("mkt")
    local_count, window, points = kernel.shape
    scenarios = quotes.shape[0]
    trades, hidden = trade_embed.shape
    rows = trades // LANES
    quarter = scen_rank.shape[0]
    peers = mkt_size * scen_size
    total = quarter * peers
    rank_row = scen_rank.reshape(1, quarter)
    ranks = [rank_row]
    for k in range(scen_size - 1, 0, -1):
        ranks.append(lax.ppermute(rank_row, "scen", [(i, (i + k) % scen_size) for i in range(scen_size)]))

    vmem = pl.BlockSpec(memory_space=pltpu.VMEM)
    hbm = pl.BlockSpec(memory_space=pl.ANY)
    fused = trade_size == 1
    if fused:
        sources = (quotes, kernel)
    else:
        first = (lax.axis_index(("trade", "scen")) * local_count).astype(jnp.int32).reshape(1)
        states = pl.pallas_call(
            states_kernel,
            out_shape=jax.ShapeDtypeStruct((local_count, scenarios, points), BF),
            in_specs=[pl.BlockSpec(memory_space=pltpu.SMEM), vmem, vmem],
            out_specs=vmem,
            name="states",
        )(first, quotes, kernel)
        sources = (lax.all_gather(states, "trade", axis=0, tiled=True),)
    list_rows = trades // (SLOTS * GROUP)
    step_rows = STEP * SLOTS * scenarios
    width = -(-(trades + scenarios + 1) // LANES) * LANES
    send = pl.pallas_call(
        functools.partial(price_kernel, fused, scen_size, local_count, total // 20, total),
        out_shape=jax.ShapeDtypeStruct((peers, 1, width), F32),
        in_specs=[vmem] * (4 + scen_size) + [hbm] * (3 + len(sources)),
        out_specs=vmem,
        scratch_shapes=[
            pltpu.VMEM(trade_embed.shape, BF),
            pltpu.VMEM(w_in.shape, BF),
            pltpu.VMEM(w_mid.shape, BF),
            *(pltpu.VMEM(source.shape, BF) for source in sources),
            pltpu.VMEM((local_count * trade_size, scenarios, hidden), F32),
            pltpu.VMEM((trades, hidden), F32),
            pltpu.VMEM((16, trades), BF),
            pltpu.VMEM((list_rows, SLOTS * GROUP, trades), BF),
            pltpu.VMEM((rows, LANES), F32),
            pltpu.VMEM((list_rows + 1, SLOTS * GROUP), jnp.int32),
            pltpu.SMEM((list_rows + 1, SLOTS * GROUP), jnp.int32),
            pltpu.VMEM((list_rows, SLOTS * GROUP), F32),
            pltpu.VMEM((trades // SLOTS + 4 * STEP, SLOTS * scenarios), F32),
            *(pltpu.VMEM((step_rows, hidden), BF) for _ in range(4)),
            pltpu.VMEM((16, trades), F32),
            pltpu.SemaphoreType.DMA((8,)),
        ],
        name="price",
    )(
        trade_block.reshape(rows, LANES),
        position.reshape(rows, LANES),
        b_mid.reshape(1, hidden),
        w_out.reshape(1, hidden),
        *ranks,
        trade_embed,
        w_in,
        w_mid,
        *sources,
    )
    got = lax.all_to_all(send, ("mkt", "scen"), split_axis=0, concat_axis=0, tiled=True).reshape(peers, width)
    sums = jnp.sum(got, axis=0)
    corner = (lax.axis_index("mkt") * scen_size, trades + lax.axis_index("scen") * quarter)
    book_pnl = lax.psum(jnp.sum(lax.dynamic_slice(got, corner, (scen_size, quarter)), axis=0), "trade")
    shortfall = lax.psum(sums[trades + scenarios], "trade")
    return (book_pnl, sums[:trades], shortfall)


def solution(mesh):
    placed = (
        P("mkt", None),
        P(("trade", "scen"), None, None),
        P("trade"),
        P("trade", None),
        P("trade"),
        P(("mkt", "scen")),
        P(),
        P(),
        P(),
        P(),
    )
    return jax.shard_map(
        local,
        mesh=mesh,
        in_specs=placed,
        out_specs=(P(("mkt", "scen")), P("trade"), P()),
        check_vma=False,
    )
```

time: 207 us -> 50.2 us (0.24)
  matrix products: 80.6 us -> 0 us
  local copies, waits for them, and re-layouts: 57.4 us -> 2.92 us
  blocking collectives: 39 us -> 0 us
  Pallas kernels: 0 us -> 20 us
  loops' own time: 10.9 us -> 0 us
  waiting for transfers between devices: 6.9 us -> 14.2 us
  starting transfers between devices: 6.02 us -> 10.8 us
    dot_general x35 -> x0, matrix products: 80.6 us -> none  [the longest x16 44.7 us: price(): jnp.dot(trade_rows, w_in, preferred_element_type=jnp.float32) + embed_float]
    gather x49 -> x0, local copies, waits for them, and re-layouts: 44.2 us -> none
    psum x1 -> x0, blocking collectives: 39 us -> none  [local(): lax.psum(-jnp.dot(weights, values, precision=lax.Precision.HIGHEST), ('mk...]
    pallas_call x0 -> x1, Pallas kernels: none -> 20 us  [local(): pl.pallas_call(functools.partial(price_kernel, fused, scen_size, local_co...]
    another operation x2 -> x0, loops' own time: 10.9 us -> none  [the longest x1 10.9 us: local(): values = lax.map(price, jnp.arange(scen_count, dtype=jnp.int32))]
    dynamic_slice x16 -> x0, local copies, waits for them, and re-layouts: 9.38 us -> none  [local(): values = lax.map(price, jnp.arange(scen_count, dtype=jnp.int32))]
    ppermute x0 -> x3, starting transfers between devices: none -> 6.09 us  [local(): lax.ppermute(rank_row, 'scen', [(i, (i + k) % scen_size) for i in range(s...]
    ppermute x0 -> x3, waiting for transfers between devices: none -> 3.78 us  [local(): lax.ppermute(rank_row, 'scen', [(i, (i + k) % scen_size) for i in range(s...]
  transfers between devices with their start and end apart: 1 -> 4, of which waited for: 1 -> 3; matrix products, arithmetic and copies ran while one was open for 1% -> 1% of each run, Pallas kernels for 0% -> 0%
where the time goes in v1:
time: 50.2 us; the launch traced here: 49.5 us
  Pallas kernels  20 us (40%)
  waiting for transfers between devices  14.2 us (28%)
  starting transfers between devices  10.8 us (22%)
  local copies, waits for them, and re-layouts  2.92 us (6%)
  other arithmetic  0.77 us (2%)
  between operations  0.68 us (1%)
    pallas_call x1, Pallas kernels, local(): pl.pallas_call(functools.partial(price_kernel, fused, scen_size, local_co...  20 us
    all_to_all x1, waiting for transfers between devices, local(): lax.all_to_all(send, ('mkt', 'scen'), split_axis=0, concat_axis=0, tiled=...  10.4 us
    ppermute x3, starting transfers between devices, local(): lax.ppermute(rank_row, 'scen', [(i, (i + k) % scen_size) for i in range(s...  6.09 us
    all_to_all x1, starting transfers between devices, local(): lax.all_to_all(send, ('mkt', 'scen'), split_axis=0, concat_axis=0, tiled=...  4.76 us
    ppermute x3, waiting for transfers between devices, local(): lax.ppermute(rank_row, 'scen', [(i, (i + k) % scen_size) for i in range(s...  3.78 us
    unnamed x10, local copies, waits for them, and re-layouts  1.17 us
  transfers between devices with their start and end apart: 4, of which 3 were waited for; matrix products, arithmetic and copies ran while one was open for 1% of the time, Pallas kernels for 0%

profile of v1, /device:TPU:0, one launch (start us, length us, event | category | flops | bytes accessed | tf_op | source)
XLA Modules:
  0.0 49.5 jit_solution(14394435450693279939)
XLA Ops:
  0.6 0.0 copy-start
  0.6 0.0 copy-start.4
  0.7 0.6 %copy-done = s32[16]{0:T(128)S(1)} copy-done((s32[16]{0:T(128)S(1)}, s32[16]{0:T(128)}, u32[]{:S(2)}) %copy-start) | copy-done | bytes 88
  1.3 5.1 %collective-permute-start = (s32[1,16]{1,0:T(1,128)S(1)}, s32[1,16]{1,0:T(1,128)S(1)}, u32[]{:S(2)}, u32[]{:S(2)}) collective-permute-start(s32[1,16]{1,0:T(1,128)S(1)} %bitcast.9), channel_id=1, source_target_pairs={{0,3},{1,0},{2,1},{3,2},{4,7},{5,4},{6,5},{7,6},{8,11},{9,8},{10,9... | collective-permute-start | bytes 200 | tf_op jit(solution)/shard_map/ppermute | solution.py:219
  6.4 0.0 collective-permute-start.1
  6.4 1.0 %collective-permute-start.2 = (s32[1,16]{1,0:T(1,128)S(1)}, s32[1,16]{1,0:T(1,128)S(1)}, u32[]{:S(2)}, u32[]{:S(2)}) collective-permute-start(s32[1,16]{1,0:T(1,128)S(1)} %bitcast.11), channel_id=1, source_target_pairs={{0,1},{1,2},{2,3},{3,0},{4,5},{5,6},{6,7},{7,4},{8,9},{9,10},{10,1... | collective-permute-start | bytes 200 | tf_op jit(solution)/shard_map/ppermute | solution.py:219
  7.4 0.0 copy-done.4
  7.4 0.6 %reshape.26.refs_3_ = bf16[1,256]{1,0:T(2,128)(2,1)} reshape(bf16[256]{0:T(256)(128)(2,1)S(1)} %copy-done.4) | data formatting | bytes 1024 | tf_op jit(solution)/shard_map/reshape | solution.py:267
  7.9 0.0 collective-permute-done.refs_5_
  8.0 0.0 copy-start.1
  8.0 2.9 %collective-permute-done.1.refs_6_ = s32[1,16]{1,0:T(1,128)S(1)} collective-permute-done((s32[1,16]{1,0:T(1,128)S(1)}, s32[1,16]{1,0:T(1,128)S(1)}, u32[]{:S(2)}, u32[]{:S(2)}) %collective-permute-start.1) | collective-permute-done | bytes 96 | tf_op jit(solution)/shard_map/ppermute | solution.py:219
  10.8 0.0 copy-start.2
  10.8 0.9 %collective-permute-done.2.refs_7_ = s32[1,16]{1,0:T(1,128)S(1)} collective-permute-done((s32[1,16]{1,0:T(1,128)S(1)}, s32[1,16]{1,0:T(1,128)S(1)}, u32[]{:S(2)}, u32[]{:S(2)}) %collective-permute-start.2) | collective-permute-done | bytes 96 | tf_op jit(solution)/shard_map/ppermute | solution.py:219
  11.7 0.0 copy-start.3
  11.7 0.0 copy-done.1
  11.7 0.0 copy-done.2
  11.7 0.5 %copy-done.3 = s32[1,16]{1,0:T(1,128)} copy-done((s32[1,16]{1,0:T(1,128)}, s32[1,16]{1,0:T(1,128)S(1)}, u32[]{:S(2)}) %copy-start.3) | copy-done | bytes 88
  12.3 20.0 %price.1 = f32[32,1,2176]{2,1,0:T(1,128)} custom-call(s32[16,128]{1,0:T(8,128)} %bitcast.5, f32[16,128]{1,0:T(8,128)} %bitcast.6, f32[1,256]{1,0:T(1,128)} %bitcast.7, bf16[1,256]{1,0:T(2,128)(2,1)} %reshape.26.refs_3_, s32[1,16]{1,0:T(1,128)} %bitcast.8, s32[1,16]{1,0:T(1,128)} %copy-done.1, s32[1,16]{1,0:T(1,128)} %copy-done.2, s32[1,16]{1,0:T(1,128)} %copy-done.3, ...), custom_call_target="tpu_custom_call" | custom-call | tf_op jit(solution)/shard_map/price/pallas_call | solution.py:239
  32.3 4.8 %all-to-all-start = ((f32[32,1,2176]{2,1,0:T(1,128)}), f32[32,1,2176]{2,1,0:T(1,128)S(1)}, u32[]{:S(2)}, u32[]{:S(2)}) async-start(f32[32,1,2176]{2,1,0:T(1,128)} %price.1), calls=%async_computation | async-start | bytes 557056 | tf_op jit(solution)/shard_map/all_to_all | solution.py:274
  37.1 10.4 %all-to-all-done = f32[32,1,2176]{2,1,0:T(1,128)S(1)} async-done(((f32[32,1,2176]{2,1,0:T(1,128)}), f32[32,1,2176]{2,1,0:T(1,128)S(1)}, u32[]{:S(2)}, u32[]{:S(2)}) %all-to-all-start) | async-done | bytes 278560 | tf_op jit(solution)/shard_map/all_to_all | solution.py:274
  47.5 0.2 reduce_sum.19
  47.7 0.6 %slice.8 = f32[2048]{0:T(1024)} slice(f32[2176]{0:T(1024)S(1)} %reduce_sum.19), slice={[0:2048]} | slice | bytes 16384 | tf_op jit(solution)/shard_map/slice | solution.py:279
  48.3 0.6 %slice.9 = f32[1]{0:T(128)} slice(f32[2176]{0:T(1024)S(1)} %reduce_sum.19), slice={[2112:2113]} | slice | bytes 8 | tf_op jit(solution)/shard_map/slice | solution.py:278
  48.9 0.6 %dynamic-slice_reduce_fusion = f32[16]{0:T(128)} fusion(f32[32,1,2176]{2,1,0:T(1,128)S(1)} %all-to-all-done, s32[]{:T(128)S(6)} %select_n.6, s32[]{:T(128)S(6)} %select_n.7), kind=kLoop, calls=%fused_computation | loop fusion | flops 48 | bytes 328 | tf_op jit(solution)/shard_map/reduce_sum | solution.py:277
Async XLA Ops:
  0.6 0.7 %copy-start = (s32[16]{0:T(128)S(1)}, s32[16]{0:T(128)}, u32[]{:S(2)}) copy-start(s32[16]{0:T(128)} %param.15) | copy-start | bytes 196
  0.6 6.7 %copy-start.4 = (bf16[256]{0:T(256)(128)(2,1)S(1)}, bf16[256]{0:T(256)(128)(2,1)}, u32[]{:S(2)}) copy-start(bf16[256]{0:T(256)(128)(2,1)} %param.19) | copy-start | bytes 1540
  1.3 6.7 %collective-permute-start = (s32[1,16]{1,0:T(1,128)S(1)}, s32[1,16]{1,0:T(1,128)S(1)}, u32[]{:S(2)}, u32[]{:S(2)}) collective-permute-start(s32[1,16]{1,0:T(1,128)S(1)} %bitcast.9), channel_id=1, source_target_pairs={{0,3},{1,0},{2,1},{3,2},{4,7},{5,4},{6,5},{7,6},{8,11},{9,8},{10,9... | collective-permute-start | bytes 200 | tf_op jit(solution)/shard_map/ppermute | solution.py:219
  6.4 4.5 %collective-permute-start.1 = (s32[1,16]{1,0:T(1,128)S(1)}, s32[1,16]{1,0:T(1,128)S(1)}, u32[]{:S(2)}, u32[]{:S(2)}) collective-permute-start(s32[1,16]{1,0:T(1,128)S(1)} %bitcast.10), channel_id=1, source_target_pairs={{0,2},{1,3},{2,0},{3,1},{4,6},{5,7},{6,4},{7,5},{8,10},{9,11},{10,... | collective-permute-start | bytes 200 | tf_op jit(solution)/shard_map/ppermute | solution.py:219
  6.4 5.4 %collective-permute-start.2 = (s32[1,16]{1,0:T(1,128)S(1)}, s32[1,16]{1,0:T(1,128)S(1)}, u32[]{:S(2)}, u32[]{:S(2)}) collective-permute-start(s32[1,16]{1,0:T(1,128)S(1)} %bitcast.11), channel_id=1, source_target_pairs={{0,1},{1,2},{2,3},{3,0},{4,5},{5,6},{6,7},{7,4},{8,9},{9,10},{10,1... | collective-permute-start | bytes 200 | tf_op jit(solution)/shard_map/ppermute | solution.py:219
  8.0 3.8 %copy-start.1 = (s32[1,16]{1,0:T(1,128)}, s32[1,16]{1,0:T(1,128)S(1)}, u32[]{:S(2)}) copy-start(s32[1,16]{1,0:T(1,128)S(1)} %collective-permute-done.refs_5_) | copy-start | bytes 196
  10.8 0.9 %copy-start.2 = (s32[1,16]{1,0:T(1,128)}, s32[1,16]{1,0:T(1,128)S(1)}, u32[]{:S(2)}) copy-start(s32[1,16]{1,0:T(1,128)S(1)} %collective-permute-done.1.refs_6_) | copy-start | bytes 196
  11.7 0.5 %copy-start.3 = (s32[1,16]{1,0:T(1,128)}, s32[1,16]{1,0:T(1,128)S(1)}, u32[]{:S(2)}) copy-start(s32[1,16]{1,0:T(1,128)S(1)} %collective-permute-done.2.refs_7_) | copy-start | bytes 196
  32.3 15.2 %all-to-all-start = ((f32[32,1,2176]{2,1,0:T(1,128)}), f32[32,1,2176]{2,1,0:T(1,128)S(1)}, u32[]{:S(2)}, u32[]{:S(2)}) async-start(f32[32,1,2176]{2,1,0:T(1,128)} %price.1), calls=%async_computation | async-start | bytes 557056 | tf_op jit(solution)/shard_map/all_to_all | solution.py:274

commit v2 on v1

v2 whole, which is shorter than its diff:
```python
import functools

import jax
import jax.numpy as jnp
from jax import lax
from jax.experimental import pallas as pl
from jax.experimental.pallas import tpu as pltpu
from jax.sharding import PartitionSpec as P

QSTEP = 8
LANES = 128
SLOTS = 4
GROUP = 256
STEP = 4
BF = jnp.bfloat16
F32 = jnp.float32
NT = (((1,), (1,)), ((), ()))
HIGH = lax.Precision.HIGHEST


def iota(shape, dim):
    return lax.broadcasted_iota(jnp.int32, shape, dim)


def split3(x):
    high = x.astype(BF)
    rest = x - high.astype(F32)
    mid = rest.astype(BF)
    low = (rest - mid.astype(F32)).astype(BF)
    return high.astype(F32), mid.astype(F32), low.astype(F32)


def build_states(first, quotes_ref, kernel_ref, emit):
    local_count, window, _ = kernel_ref.shape
    quote_count = quotes_ref.shape[1]
    lane = iota((1, window), 1)
    for j in range(local_count):
        start = jnp.clip(QSTEP * (first + j) - (window - QSTEP) // 2, 0, quote_count - window)
        tile = start // window
        back = window - (start - tile * window)
        after = jnp.minimum(tile + 1, quote_count // window - 1)
        low = quotes_ref[:, pl.ds(pl.multiple_of(tile * window, window), window)].astype(F32)
        high = quotes_ref[:, pl.ds(pl.multiple_of(after * window, window), window)].astype(F32)
        cut = jnp.where(lane < back, pltpu.roll(low, back, 1), pltpu.roll(high, back, 1)).astype(BF)
        emit(j, jnp.dot(cut, kernel_ref[j], preferred_element_type=F32).astype(BF))


def states_kernel(first_ref, quotes_ref, kernel_ref, out_ref):
    def emit(j, state):
        out_ref[j] = state

    build_states(first_ref[0], quotes_ref, kernel_ref, emit)


def lanes_of(table, index):
    return jnp.take_along_axis(table, index, axis=1)


def price_kernel(fused, scen_size, local_count, span, total, *refs):
    rank_refs, refs = refs[:scen_size], refs[scen_size:]
    loaded = 9 if fused else 8
    origin, (send_ref, *refs) = refs[:loaded], refs[loaded:]
    copies, refs = refs[:loaded], refs[loaded:]
    block_ref, position_ref, *sources, w_in_ref, embed_ref, b_mid_ref, w_mid_ref, w_out_ref = copies
    pre_ref, embed32_ref, index_ref, index_smem, weighted_ref, value_ref, first_a, first_b, second_a, second_b, sems = refs
    loads = [pltpu.make_async_copy(here, there, sems.at[n]) for n, (here, there) in enumerate(zip(origin, copies))]
    for load in loads:
        load.start()
    rows = block_ref.shape[0]
    trades = rows * LANES
    _, scenarios, hidden = pre_ref.shape
    tile_rows = SLOTS * scenarios
    z = lax.axis_index("scen")
    loads[0].wait()
    loads[1].wait()

    block = block_ref[...]
    group = block // local_count
    mine = group % scen_size == z
    slot = (group // scen_size) * local_count + block % local_count
    flag = jnp.where(mine, 1.0, 0.0).astype(BF)
    upper = jnp.where(iota((LANES, LANES), 0) <= iota((LANES, LANES), 1), 1.0, 0.0).astype(BF)
    lower = jnp.where(iota((rows, rows), 0) > iota((rows, rows), 1), 1.0, 0.0).astype(BF)
    upto = jnp.dot(flag, upper, preferred_element_type=F32)
    above = jnp.sum(jnp.dot(lower, flag, preferred_element_type=F32), axis=1, keepdims=True)
    through = (above + upto[:, LANES - 1 :]).astype(jnp.int32)
    place = (upto + above).astype(jnp.int32) - 1
    above = above.astype(jnp.int32)
    count = jnp.sum(flag.astype(F32)).astype(jnp.int32)
    lane = iota((rows, LANES), 1)
    line = iota((rows, LANES), 0)
    want = (lane + 1).astype(F32)
    found = jnp.zeros((rows, LANES), jnp.int32)
    bit = LANES // 2
    while bit:
        found = jnp.where(lanes_of(upto, found + (bit - 1)) < want, found + bit, found)
        bit //= 2
    entry = lanes_of(slot, found) * trades + line * LANES + found
    placed = lanes_of(position_ref[...], found)
    cuts = rows // SLOTS
    spot = ((line % cuts) * LANES + lane) * SLOTS + line // cuts
    listed, weighted = jnp.zeros((rows, LANES), jnp.int32), jnp.zeros((rows, LANES), F32)
    for r in range(rows):
        one = slice(r, r + 1)
        here = (spot >= above[one]) & (spot < through[one])
        at = (spot - above[one]) & (LANES - 1)
        listed = jnp.where(here, lanes_of(jnp.broadcast_to(entry[one], (rows, LANES)), at), listed)
        weighted = jnp.where(here, lanes_of(jnp.broadcast_to(placed[one], (rows, LANES)), at), weighted)
    index_ref[:rows, :] = listed
    weighted_ref[...] = weighted
    index_ref[rows:, :] = jnp.zeros((8, LANES), jnp.int32)
    copy = pltpu.make_async_copy(index_ref, index_smem, sems.at[loaded])
    copy.start()
    for load in loads[2:-4]:
        load.wait()

    w_in = w_in_ref[...] * BF(0.5)

    def emit(j, state):
        pre_ref[j] = jnp.dot(state, w_in, preferred_element_type=F32)

    if fused:
        build_states(z * local_count, *sources, emit)
    else:

        def each(j, carry):
            emit(j, sources[0][j])
            return carry

        lax.fori_loop(0, sources[0].shape[0], each, 0)
    for load in loads[-4:]:
        load.wait()
    embed32_ref[...] = embed_ref[...].astype(F32) * 0.5
    value_ref[...] = jnp.zeros_like(value_ref)
    w_mid_ref[...] = w_mid_ref[...] * BF(0.5)
    bias = b_mid_ref[...] * 0.5
    w_out = jnp.broadcast_to(w_out_ref[...].reshape(1, hidden), (16, hidden))
    copy.wait()

    def first_stage(step, out_ref):
        for t in range(STEP):
            tile = step * STEP + t
            for k in range(SLOTS):
                chosen = index_smem[k * cuts + tile // LANES, tile % LANES]
                half = pre_ref[chosen // trades] + embed32_ref[pl.ds(chosen % trades, 1), :]
                at = (t * SLOTS + k) * scenarios
                out_ref[at : at + scenarios, :] = (half * (jnp.tanh(half) + 1.0)).astype(BF)

    def second_stage(in_ref, out_ref):
        for t in range(STEP):
            at = slice(t * tile_rows, (t + 1) * tile_rows)
            half = jnp.dot(in_ref[at, :], w_mid_ref[...], preferred_element_type=F32) + bias
            out_ref[at, :] = (half * (jnp.tanh(half) + 1.0)).astype(BF)

    def third_stage(step, in_ref):
        for t in range(STEP):
            at = slice(t * tile_rows, (t + 1) * tile_rows)
            value = lax.dot_general(w_out, in_ref[at, :], NT, preferred_element_type=F32)
            value_ref[pl.ds(step * STEP + t, 1), :] = value[0:1]

    def price(pair, carry):
        first_stage(2 * pair, first_a)
        second_stage(first_b, second_b)
        third_stage(2 * pair, second_a)
        first_stage(2 * pair + 1, first_b)
        second_stage(first_a, second_a)
        third_stage(2 * pair + 1, second_b)
        return carry

    steps = pl.cdiv(count, SLOTS * STEP)
    lax.fori_loop(0, pl.cdiv(steps + 2, 2), price, 0)

    ranks = jnp.concatenate([ref[...] for ref in rank_refs] * SLOTS, axis=1).astype(F32)
    weight_sum = jnp.sum(jnp.exp(-iota((8, total), 1).astype(F32) / span), axis=1, keepdims=True)[0:1]
    weight = pltpu.roll(jnp.exp(-ranks / span) / weight_sum, z * rank_refs[0].shape[1], 1)
    own = iota((8, tile_rows), 0) == iota((8, tile_rows), 1) // scenarios
    weights = jnp.where(own, jnp.broadcast_to(weight, (8, tile_rows)), 0.0)

    def weigh(b, carry):
        tail, book = carry
        value = value_ref[pl.ds(pl.multiple_of(b * GROUP + 2 * STEP, 8), GROUP), :]
        sums = lax.dot_general(weights, value, NT, precision=HIGH, preferred_element_type=F32)
        tile = place // SLOTS - b * GROUP
        for k in range(SLOTS):
            for j in range(GROUP // LANES):
                row = jnp.broadcast_to(sums[k : k + 1, j * LANES : (j + 1) * LANES], (rows, LANES))
                here = (place % SLOTS == k) & (tile // LANES == j) & mine
                tail = jnp.where(here, lanes_of(row, tile % LANES), tail)
        take = [
            jnp.concatenate([weighted_ref[pl.ds(k * cuts + b * (GROUP // LANES) + j, 1), :] for j in range(GROUP // LANES)], axis=1)
            for k in range(SLOTS)
        ]
        placed = jnp.concatenate([*take, jnp.zeros((8 - SLOTS, GROUP), F32)], axis=0)
        return tail, book + jnp.dot(placed, value, precision=HIGH, preferred_element_type=F32)

    tail, book = lax.fori_loop(
        0, pl.cdiv(count, SLOTS * GROUP), weigh, (jnp.zeros((rows, LANES), F32), jnp.zeros((8, tile_rows), F32))
    )
    book = jnp.sum(jnp.where(own, book, 0.0), axis=0, keepdims=True)
    loss = -jnp.sum(book * weight, axis=1, keepdims=True)
    book = sum(book[:, k * scenarios : (k + 1) * scenarios] for k in range(SLOTS))
    book = jnp.concatenate([book, loss, jnp.zeros((1, LANES - scenarios - 1), F32)], axis=1)
    out = jnp.concatenate([-tail, *split3(book), jnp.zeros((5, LANES), F32)], axis=0).astype(BF)
    for p in range(send_ref.shape[0]):
        send_ref[p] = out


def total_kernel(scen_size, quarter, got_ref, book_ref, marginal_ref, loss_ref):
    rows = marginal_ref.shape[0]
    scenarios = scen_size * quarter
    sums = jnp.sum(got_ref[...].astype(F32), axis=0)
    marginal_ref[...] = sums[:rows]
    book = got_ref[pl.ds(lax.axis_index("mkt") * scen_size, scen_size)].astype(F32)
    book = jnp.sum(jnp.sum(book, axis=0)[rows:], axis=0, keepdims=True)
    back = LANES - lax.axis_index("scen") * quarter
    book_ref[...] = pltpu.roll(book, back, 1)[:, :quarter]
    loss_ref[...] = jnp.sum(sums[rows:, scenarios : scenarios + 1], axis=0, keepdims=True)


def local(quotes, kernel, trade_block, trade_embed, position, scen_rank, w_in, w_mid, b_mid, w_out):
    trade_size, scen_size, mkt_size = lax.axis_size("trade"), lax.axis_size("scen"), lax.axis_size("mkt")
    local_count, window, points = kernel.shape
    scenarios = quotes.shape[0]
    trades, hidden = trade_embed.shape
    rows = trades // LANES
    quarter = scen_rank.shape[0]
    peers = mkt_size * scen_size
    total = quarter * peers
    rank_row = scen_rank.reshape(1, quarter)
    ranks = [rank_row]
    for k in range(scen_size - 1, 0, -1):
        ranks.append(lax.ppermute(rank_row, "scen", [(i, (i + k) % scen_size) for i in range(scen_size)]))

    vmem = pl.BlockSpec(memory_space=pltpu.VMEM)
    smem = pl.BlockSpec(memory_space=pltpu.SMEM)

    hbm = pl.BlockSpec(memory_space=pl.ANY)

    def held(x):
        return pltpu.with_memory_space_constraint(x, pltpu.VMEM)

    fused = trade_size == 1
    if fused:
        sources = (quotes, kernel)
    else:
        first = (lax.axis_index(("trade", "scen")) * local_count).astype(jnp.int32).reshape(1)
        states = pl.pallas_call(
            states_kernel,
            out_shape=jax.ShapeDtypeStruct((local_count, scenarios, points), BF),
            in_specs=[smem, vmem, vmem],
            out_specs=vmem,
            name="states",
        )(first, quotes, kernel)
        sources = (lax.all_gather(states, "trade", axis=0, tiled=True),)
    step_rows = STEP * SLOTS * scenarios
    tiles = -(-(trades // SLOTS + 4 * STEP) // LANES) * LANES
    inputs = (
        trade_block.reshape(rows, LANES), position.reshape(rows, LANES), *sources, w_in, trade_embed,
        b_mid.reshape(1, hidden), w_mid, w_out,
    )
    send = pl.pallas_call(
        functools.partial(price_kernel, fused, scen_size, local_count, total // 20, total),
        out_shape=pltpu.VMEM((peers, rows + 8, LANES), BF),
        in_specs=[vmem] * scen_size + [hbm] * len(inputs),
        out_specs=vmem,
        scratch_shapes=[
            *(pltpu.VMEM(x.shape, x.dtype) for x in inputs),
            pltpu.VMEM((local_count * trade_size, scenarios, hidden), F32),
            pltpu.VMEM((trades, hidden), F32),
            pltpu.VMEM((rows + 8, LANES), jnp.int32),
            pltpu.SMEM((rows + 8, LANES), jnp.int32),
            pltpu.VMEM((rows, LANES), F32),
            pltpu.VMEM((tiles, SLOTS * scenarios), F32),
            *(pltpu.VMEM((step_rows, hidden), BF) for _ in range(4)),
            pltpu.SemaphoreType.DMA((len(inputs) + 1,)),
        ],
        name="price",
    )(*(held(rank) for rank in ranks), *inputs)
    got = lax.all_to_all(send, ("mkt", "scen"), split_axis=0, concat_axis=0, tiled=True)
    book_pnl, marginal, shortfall = pl.pallas_call(
        functools.partial(total_kernel, scen_size, quarter),
        out_shape=(
            jax.ShapeDtypeStruct((1, quarter), F32),
            jax.ShapeDtypeStruct((rows, LANES), F32),
            jax.ShapeDtypeStruct((1, 1), F32),
        ),
        in_specs=[vmem],
        out_specs=(vmem, vmem, vmem),
        name="total",
    )(held(got))
    book_pnl = lax.psum(book_pnl.reshape(quarter), "trade")
    shortfall = lax.psum(shortfall.reshape(()), "trade")
    return (book_pnl, marginal.reshape(trades), shortfall)


def solution(mesh):
    placed = (
        P("mkt", None),
        P(("trade", "scen"), None, None),
        P("trade"),
        P("trade", None),
        P("trade"),
        P(("mkt", "scen")),
        P(),
        P(),
        P(),
        P(),
    )
    return jax.shard_map(
        local,
        mesh=mesh,
        in_specs=placed,
        out_specs=(P(("mkt", "scen")), P("trade"), P()),
        check_vma=False,
    )
```

time: 50.2 us -> 43.6 us (0.87)
  blocking collectives: 0 us -> 13.7 us
  waiting for transfers between devices: 14.2 us -> 2.22 us
  starting transfers between devices: 10.8 us -> 6.99 us
  local copies, waits for them, and re-layouts: 2.92 us -> 0.65 us
  Pallas kernels: 20 us -> 19.1 us
  other arithmetic: 0.77 us -> 0 us
    all_to_all x0 -> x1, blocking collectives: none -> 13.7 us  [local(): lax.all_to_all(send, ('mkt', 'scen'), split_axis=0, concat_axis=0, tiled=...]
    all_to_all x1 -> x0, waiting for transfers between devices: 10.4 us -> none  [local(): lax.all_to_all(send, ('mkt', 'scen'), split_axis=0, concat_axis=0, tiled=...]
    all_to_all x1 -> x0, starting transfers between devices: 4.76 us -> none  [local(): lax.all_to_all(send, ('mkt', 'scen'), split_axis=0, concat_axis=0, tiled=...]
    ppermute x3, waiting for transfers between devices: 3.78 us -> 2.22 us  [local(): lax.ppermute(rank_row, 'scen', [(i, (i + k) % scen_size) for i in range(s...]
    pallas_call x1, Pallas kernels: 20 us -> 18.5 us  [local(): pl.pallas_call(functools.partial(price_kernel, fused, scen_size, local_co...]
    slice x2 -> x0, local copies, waits for them, and re-layouts: 1.18 us -> none  [the longest x1 0.6 us: local(): return (book_pnl, sums[:trades], shortfall)]
    ppermute x3, starting transfers between devices: 6.09 us -> 6.99 us  [local(): lax.ppermute(rank_row, 'scen', [(i, (i + k) % scen_size) for i in range(s...]
    reduce_sum x2 -> x0, other arithmetic: 0.77 us -> none  [the longest x1 0.6 us: local(): jnp.sum(lax.dynamic_slice(got, corner, (scen_size, quarter)), axis=0)]
  transfers between devices with their start and end apart: 4 -> 3, of which waited for: 3 -> 2; matrix products, arithmetic and copies ran while one was open for 1% -> 0% of each run, Pallas kernels for 0% -> 0%
where the time goes in v2:
time: 43.6 us; the launch traced here: 43.3 us
  Pallas kernels  19.1 us (44%)
  blocking collectives  13.7 us (31%)
  starting transfers between devices  6.99 us (16%)
  waiting for transfers between devices  2.22 us (5%)
  local copies, waits for them, and re-layouts  0.65 us (1%)
  between operations  0.65 us (1%)
    pallas_call x1, Pallas kernels, local(): pl.pallas_call(functools.partial(price_kernel, fused, scen_size, local_co...  18.5 us
    all_to_all x1, blocking collectives, local(): lax.all_to_all(send, ('mkt', 'scen'), split_axis=0, concat_axis=0, tiled=...  13.7 us
    ppermute x3, starting transfers between devices, local(): lax.ppermute(rank_row, 'scen', [(i, (i + k) % scen_size) for i in range(s...  6.99 us
    ppermute x3, waiting for transfers between devices, local(): lax.ppermute(rank_row, 'scen', [(i, (i + k) % scen_size) for i in range(s...  2.22 us
  transfers between devices with their start and end apart: 3, of which 2 were waited for; matrix products, arithmetic and copies ran while one was open for 0% of the time, Pallas kernels for 0%

profile of v2, /device:TPU:0, one launch (start us, length us, event | category | flops | bytes accessed | tf_op | source)
XLA Modules:
  0.0 43.3 jit_solution(2820707239342151269)
XLA Ops:
  0.6 0.0 copy-start
  0.6 0.6 %copy-done = s32[16]{0:T(128)S(1)} copy-done((s32[16]{0:T(128)S(1)}, s32[16]{0:T(128)}, u32[]{:S(2)}) %copy-start) | copy-done | bytes 88
  1.3 3.1 %collective-permute-start.2 = (s32[1,16]{1,0:T(1,128)S(1)}, s32[1,16]{1,0:T(1,128)S(1)}, u32[]{:S(2)}, u32[]{:S(2)}) collective-permute-start(s32[1,16]{1,0:T(1,128)S(1)} %bitcast.7), channel_id=1, source_target_pairs={{0,1},{1,2},{2,3},{3,0},{4,5},{5,6},{6,7},{7,4},{8,9},{9,10},{10,1... | collective-permute-start | bytes 200 | tf_op jit(solution)/shard_map/ppermute | solution.py:232
  4.3 2.6 %collective-permute-start.1 = (s32[1,16]{1,0:T(1,128)S(1)}, s32[1,16]{1,0:T(1,128)S(1)}, u32[]{:S(2)}, u32[]{:S(2)}) collective-permute-start(s32[1,16]{1,0:T(1,128)S(1)} %bitcast.8), channel_id=1, source_target_pairs={{0,2},{1,3},{2,0},{3,1},{4,6},{5,7},{6,4},{7,5},{8,10},{9,11},{10,... | collective-permute-start | bytes 200 | tf_op jit(solution)/shard_map/ppermute | solution.py:232
  6.9 1.3 %collective-permute-start = (s32[1,16]{1,0:T(1,128)S(1)}, s32[1,16]{1,0:T(1,128)S(1)}, u32[]{:S(2)}, u32[]{:S(2)}) collective-permute-start(s32[1,16]{1,0:T(1,128)S(1)} %bitcast.9), channel_id=1, source_target_pairs={{0,3},{1,0},{2,1},{3,2},{4,7},{5,4},{6,5},{7,6},{8,11},{9,8},{10,9... | collective-permute-start | bytes 200 | tf_op jit(solution)/shard_map/ppermute | solution.py:232
  8.3 0.0 collective-permute-done.2.refs_3_
  8.3 0.5 %collective-permute-done.1.refs_2_ = s32[1,16]{1,0:T(1,128)S(1)} collective-permute-done((s32[1,16]{1,0:T(1,128)S(1)}, s32[1,16]{1,0:T(1,128)S(1)}, u32[]{:S(2)}, u32[]{:S(2)}) %collective-permute-start.1) | collective-permute-done | bytes 96 | tf_op jit(solution)/shard_map/ppermute | solution.py:232
  8.8 1.7 %collective-permute-done.refs_1_ = s32[1,16]{1,0:T(1,128)S(1)} collective-permute-done((s32[1,16]{1,0:T(1,128)S(1)}, s32[1,16]{1,0:T(1,128)S(1)}, u32[]{:S(2)}, u32[]{:S(2)}) %collective-permute-start) | collective-permute-done | bytes 96 | tf_op jit(solution)/shard_map/ppermute | solution.py:232
  10.5 18.5 %price.1 = bf16[32,24,128]{2,1,0:T(8,128)(2,1)S(1)} custom-call(s32[1,16]{1,0:T(1,128)S(1)} %bitcast.10, s32[1,16]{1,0:T(1,128)S(1)} %collective-permute-done.refs_1_, s32[1,16]{1,0:T(1,128)S(1)} %collective-permute-done.1.refs_2_, s32[1,16]{1,0:T(1,128)S(1)} %collective-permute-done.2.refs_3_, s32[16,128]{1,0:T(8,128)} %bitcast.11, f32[16,128]{1,0:T(8,128)} %bitcast.12, ...), custom_call_target="tpu_custom_call" | custom-call | tf_op jit(solution)/shard_map/price/pallas_call | solution.py:261
  29.0 13.7 %all_to_all.5.got_ref = bf16[32,24,128]{2,1,0:T(8,128)(2,1)S(1)} all-to-all(bf16[32,24,128]{2,1,0:T(8,128)(2,1)S(1)} %price.1), channel_id=1, replica_groups=mesh['mkt'=8,'trade'=1,'scen'=4] {'mkt','scen'}, dimensions={0} | all-to-all | bytes 393216 | tf_op jit(solution)/shard_map/all_to_all | solution.py:279
  42.7 0.6 %total.1 = (f32[1,16]{1,0:T(1,128)}, f32[16,128]{1,0:T(8,128)}, f32[1,1]{1,0:T(1,128)}) custom-call(bf16[32,24,128]{2,1,0:T(8,128)(2,1)S(1)} %all_to_all.5.got_ref), custom_call_target="tpu_custom_call" | custom-call | tf_op jit(solution)/shard_map/total/pallas_call | solution.py:280
Async XLA Ops:
  0.6 0.7 %copy-start = (s32[16]{0:T(128)S(1)}, s32[16]{0:T(128)}, u32[]{:S(2)}) copy-start(s32[16]{0:T(128)} %param.15) | copy-start | bytes 196
  1.3 7.0 %collective-permute-start.2 = (s32[1,16]{1,0:T(1,128)S(1)}, s32[1,16]{1,0:T(1,128)S(1)}, u32[]{:S(2)}, u32[]{:S(2)}) collective-permute-start(s32[1,16]{1,0:T(1,128)S(1)} %bitcast.7), channel_id=1, source_target_pairs={{0,1},{1,2},{2,3},{3,0},{4,5},{5,6},{6,7},{7,4},{8,9},{9,10},{10,1... | collective-permute-start | bytes 200 | tf_op jit(solution)/shard_map/ppermute | solution.py:232
  4.3 4.5 %collective-permute-start.1 = (s32[1,16]{1,0:T(1,128)S(1)}, s32[1,16]{1,0:T(1,128)S(1)}, u32[]{:S(2)}, u32[]{:S(2)}) collective-permute-start(s32[1,16]{1,0:T(1,128)S(1)} %bitcast.8), channel_id=1, source_target_pairs={{0,2},{1,3},{2,0},{3,1},{4,6},{5,7},{6,4},{7,5},{8,10},{9,11},{10,... | collective-permute-start | bytes 200 | tf_op jit(solution)/shard_map/ppermute | solution.py:232
  6.9 3.6 %collective-permute-start = (s32[1,16]{1,0:T(1,128)S(1)}, s32[1,16]{1,0:T(1,128)S(1)}, u32[]{:S(2)}, u32[]{:S(2)}) collective-permute-start(s32[1,16]{1,0:T(1,128)S(1)} %bitcast.9), channel_id=1, source_target_pairs={{0,3},{1,0},{2,1},{3,2},{4,7},{5,4},{6,5},{7,6},{8,11},{9,8},{10,9... | collective-permute-start | bytes 200 | tf_op jit(solution)/shard_map/ppermute | solution.py:232

commit v3 on v2

--- a/solution.py
+++ b/solution.py
@@ -11,7 +11,7 @@
 LANES = 128
 SLOTS = 4
 GROUP = 256
-STEP = 4
+STEP = 8
 BF = jnp.bfloat16
 F32 = jnp.float32
 NT = (((1,), (1,)), ((), ()))
@@ -147,28 +147,33 @@
                 out_ref[at : at + scenarios, :] = (half * (jnp.tanh(half) + 1.0)).astype(BF)
 
     def second_stage(in_ref, out_ref):
+        halves = jnp.dot(in_ref[...], w_mid_ref[...], preferred_element_type=F32)
         for t in range(STEP):
             at = slice(t * tile_rows, (t + 1) * tile_rows)
-            half = jnp.dot(in_ref[at, :], w_mid_ref[...], preferred_element_type=F32) + bias
+            half = halves[at] + bias
             out_ref[at, :] = (half * (jnp.tanh(half) + 1.0)).astype(BF)
 
     def third_stage(step, in_ref):
         for t in range(STEP):
             at = slice(t * tile_rows, (t + 1) * tile_rows)
             value = lax.dot_general(w_out, in_ref[at, :], NT, preferred_element_type=F32)
-            value_ref[pl.ds(step * STEP + t, 1), :] = value[0:1]
+            value_ref[pl.ds((step + 1) * STEP + t, 1), :] = value[0:1]
 
     def price(pair, carry):
-        first_stage(2 * pair, first_a)
+        first_stage(2 * pair + 1, first_b)
+        second_stage(first_a, second_a)
+        third_stage(2 * pair - 1, second_b)
+        first_stage(2 * pair + 2, first_a)
         second_stage(first_b, second_b)
         third_stage(2 * pair, second_a)
-        first_stage(2 * pair + 1, first_b)
-        second_stage(first_a, second_a)
-        third_stage(2 * pair + 1, second_b)
         return carry
 
-    steps = pl.cdiv(count, SLOTS * STEP)
-    lax.fori_loop(0, pl.cdiv(steps + 2, 2), price, 0)
+    pairs = pl.cdiv(count, SLOTS * STEP) // 2
+    first_stage(0, first_a)
+    lax.fori_loop(0, pairs, price, 0)
+    second_stage(first_a, second_a)
+    third_stage(2 * pairs - 1, second_b)
+    third_stage(2 * pairs, second_a)
 
     ranks = jnp.concatenate([ref[...] for ref in rank_refs] * SLOTS, axis=1).astype(F32)
     weight_sum = jnp.sum(jnp.exp(-iota((8, total), 1).astype(F32) / span), axis=1, keepdims=True)[0:1]
@@ -178,7 +183,7 @@
 
     def weigh(b, carry):
         tail, book = carry
-        value = value_ref[pl.ds(pl.multiple_of(b * GROUP + 2 * STEP, 8), GROUP), :]
+        value = value_ref[pl.ds(pl.multiple_of(b * GROUP + STEP, 8), GROUP), :]
         sums = lax.dot_general(weights, value, NT, precision=HIGH, preferred_element_type=F32)
         tile = place // SLOTS - b * GROUP
         for k in range(SLOTS):

time: 43.6 us -> 41.5 us (0.952)
  Pallas kernels: 19.1 us -> 16.3 us
  blocking collectives: 13.7 us -> 14.5 us
    pallas_call x1, Pallas kernels: 18.5 us -> 15.6 us  [local(): pl.pallas_call(functools.partial(price_kernel, fused, scen_size, local_co...]
    all_to_all x1, blocking collectives: 13.7 us -> 14.5 us  [local(): lax.all_to_all(send, ('mkt', 'scen'), split_axis=0, concat_axis=0, tiled=...]
where the time goes in v3:
time: 41.5 us; the launch traced here: 41.3 us
  Pallas kernels  16.3 us (39%)
  blocking collectives  14.5 us (35%)
  starting transfers between devices  6.99 us (17%)
  waiting for transfers between devices  2.22 us (5%)
  local copies, waits for them, and re-layouts  0.65 us (2%)
  between operations  0.65 us (2%)
    pallas_call x1, Pallas kernels, local(): pl.pallas_call(functools.partial(price_kernel, fused, scen_size, local_co...  15.6 us
    all_to_all x1, blocking collectives, local(): lax.all_to_all(send, ('mkt', 'scen'), split_axis=0, concat_axis=0, tiled=...  14.5 us
    ppermute x3, starting transfers between devices, local(): lax.ppermute(rank_row, 'scen', [(i, (i + k) % scen_size) for i in range(s...  6.99 us
    ppermute x3, waiting for transfers between devices, local(): lax.ppermute(rank_row, 'scen', [(i, (i + k) % scen_size) for i in range(s...  2.22 us
  transfers between devices with their start and end apart: 3, of which 2 were waited for; matrix products, arithmetic and copies ran while one was open for 0% of the time, Pallas kernels for 0%

profile of v3, /device:TPU:0, one launch (start us, length us, event | category | flops | bytes accessed | tf_op | source)
XLA Modules:
  0.0 41.3 jit_solution(6986083840495907405)
XLA Ops:
  0.6 0.0 copy-start
  0.6 0.6 %copy-done = s32[16]{0:T(128)S(1)} copy-done((s32[16]{0:T(128)S(1)}, s32[16]{0:T(128)}, u32[]{:S(2)}) %copy-start) | copy-done | bytes 88
  1.3 3.1 %collective-permute-start.2 = (s32[1,16]{1,0:T(1,128)S(1)}, s32[1,16]{1,0:T(1,128)S(1)}, u32[]{:S(2)}, u32[]{:S(2)}) collective-permute-start(s32[1,16]{1,0:T(1,128)S(1)} %bitcast.7), channel_id=1, source_target_pairs={{0,1},{1,2},{2,3},{3,0},{4,5},{5,6},{6,7},{7,4},{8,9},{9,10},{10,1... | collective-permute-start | bytes 200 | tf_op jit(solution)/shard_map/ppermute | solution.py:237
  4.3 2.6 %collective-permute-start.1 = (s32[1,16]{1,0:T(1,128)S(1)}, s32[1,16]{1,0:T(1,128)S(1)}, u32[]{:S(2)}, u32[]{:S(2)}) collective-permute-start(s32[1,16]{1,0:T(1,128)S(1)} %bitcast.8), channel_id=1, source_target_pairs={{0,2},{1,3},{2,0},{3,1},{4,6},{5,7},{6,4},{7,5},{8,10},{9,11},{10,... | collective-permute-start | bytes 200 | tf_op jit(solution)/shard_map/ppermute | solution.py:237
  6.9 1.3 %collective-permute-start = (s32[1,16]{1,0:T(1,128)S(1)}, s32[1,16]{1,0:T(1,128)S(1)}, u32[]{:S(2)}, u32[]{:S(2)}) collective-permute-start(s32[1,16]{1,0:T(1,128)S(1)} %bitcast.9), channel_id=1, source_target_pairs={{0,3},{1,0},{2,1},{3,2},{4,7},{5,4},{6,5},{7,6},{8,11},{9,8},{10,9... | collective-permute-start | bytes 200 | tf_op jit(solution)/shard_map/ppermute | solution.py:237
  8.3 0.0 collective-permute-done.2.refs_3_
  8.3 0.5 %collective-permute-done.1.refs_2_ = s32[1,16]{1,0:T(1,128)S(1)} collective-permute-done((s32[1,16]{1,0:T(1,128)S(1)}, s32[1,16]{1,0:T(1,128)S(1)}, u32[]{:S(2)}, u32[]{:S(2)}) %collective-permute-start.1) | collective-permute-done | bytes 96 | tf_op jit(solution)/shard_map/ppermute | solution.py:237
  8.8 1.7 %collective-permute-done.refs_1_ = s32[1,16]{1,0:T(1,128)S(1)} collective-permute-done((s32[1,16]{1,0:T(1,128)S(1)}, s32[1,16]{1,0:T(1,128)S(1)}, u32[]{:S(2)}, u32[]{:S(2)}) %collective-permute-start) | collective-permute-done | bytes 96 | tf_op jit(solution)/shard_map/ppermute | solution.py:237
  10.5 15.6 %price.1 = bf16[32,24,128]{2,1,0:T(8,128)(2,1)S(1)} custom-call(s32[1,16]{1,0:T(1,128)S(1)} %bitcast.10, s32[1,16]{1,0:T(1,128)S(1)} %collective-permute-done.refs_1_, s32[1,16]{1,0:T(1,128)S(1)} %collective-permute-done.1.refs_2_, s32[1,16]{1,0:T(1,128)S(1)} %collective-permute-done.2.refs_3_, s32[16,128]{1,0:T(8,128)} %bitcast.11, f32[16,128]{1,0:T(8,128)} %bitcast.12, ...), custom_call_target="tpu_custom_call" | custom-call | tf_op jit(solution)/shard_map/price/pallas_call | solution.py:266
  26.1 14.5 %all_to_all.5.got_ref = bf16[32,24,128]{2,1,0:T(8,128)(2,1)S(1)} all-to-all(bf16[32,24,128]{2,1,0:T(8,128)(2,1)S(1)} %price.1), channel_id=1, replica_groups=mesh['mkt'=8,'trade'=1,'scen'=4] {'mkt','scen'}, dimensions={0} | all-to-all | bytes 393216 | tf_op jit(solution)/shard_map/all_to_all | solution.py:284
  40.7 0.6 %total.1 = (f32[1,16]{1,0:T(1,128)}, f32[16,128]{1,0:T(8,128)}, f32[1,1]{1,0:T(1,128)}) custom-call(bf16[32,24,128]{2,1,0:T(8,128)(2,1)S(1)} %all_to_all.5.got_ref), custom_call_target="tpu_custom_call" | custom-call | tf_op jit(solution)/shard_map/total/pallas_call | solution.py:285
Async XLA Ops:
  0.6 0.7 %copy-start = (s32[16]{0:T(128)S(1)}, s32[16]{0:T(128)}, u32[]{:S(2)}) copy-start(s32[16]{0:T(128)} %param.15) | copy-start | bytes 196
  1.3 7.0 %collective-permute-start.2 = (s32[1,16]{1,0:T(1,128)S(1)}, s32[1,16]{1,0:T(1,128)S(1)}, u32[]{:S(2)}, u32[]{:S(2)}) collective-permute-start(s32[1,16]{1,0:T(1,128)S(1)} %bitcast.7), channel_id=1, source_target_pairs={{0,1},{1,2},{2,3},{3,0},{4,5},{5,6},{6,7},{7,4},{8,9},{9,10},{10,1... | collective-permute-start | bytes 200 | tf_op jit(solution)/shard_map/ppermute | solution.py:237
  4.3 4.5 %collective-permute-start.1 = (s32[1,16]{1,0:T(1,128)S(1)}, s32[1,16]{1,0:T(1,128)S(1)}, u32[]{:S(2)}, u32[]{:S(2)}) collective-permute-start(s32[1,16]{1,0:T(1,128)S(1)} %bitcast.8), channel_id=1, source_target_pairs={{0,2},{1,3},{2,0},{3,1},{4,6},{5,7},{6,4},{7,5},{8,10},{9,11},{10,... | collective-permute-start | bytes 200 | tf_op jit(solution)/shard_map/ppermute | solution.py:237
  6.9 3.6 %collective-permute-start = (s32[1,16]{1,0:T(1,128)S(1)}, s32[1,16]{1,0:T(1,128)S(1)}, u32[]{:S(2)}, u32[]{:S(2)}) collective-permute-start(s32[1,16]{1,0:T(1,128)S(1)} %bitcast.9), channel_id=1, source_target_pairs={{0,3},{1,0},{2,1},{3,2},{4,7},{5,4},{6,5},{7,6},{8,11},{9,8},{10,9... | collective-permute-start | bytes 200 | tf_op jit(solution)/shard_map/ppermute | solution.py:237

commit v4 on v3

--- a/solution.py
+++ b/solution.py
@@ -56,13 +56,12 @@
     return jnp.take_along_axis(table, index, axis=1)
 
 
-def price_kernel(fused, scen_size, local_count, span, total, *refs):
-    rank_refs, refs = refs[:scen_size], refs[scen_size:]
+def price_kernel(fused, scen_size, local_count, *refs):
     loaded = 9 if fused else 8
-    origin, (send_ref, *refs) = refs[:loaded], refs[loaded:]
+    origin, (value_ref, weighted_ref, place_ref, *refs) = refs[:loaded], refs[loaded:]
     copies, refs = refs[:loaded], refs[loaded:]
     block_ref, position_ref, *sources, w_in_ref, embed_ref, b_mid_ref, w_mid_ref, w_out_ref = copies
-    pre_ref, embed32_ref, index_ref, index_smem, weighted_ref, value_ref, first_a, first_b, second_a, second_b, sems = refs
+    pre_ref, embed32_ref, index_ref, index_smem, first_a, first_b, second_a, second_b, sems = refs
     loads = [pltpu.make_async_copy(here, there, sems.at[n]) for n, (here, there) in enumerate(zip(origin, copies))]
     for load in loads:
         load.start()
@@ -84,7 +83,7 @@
     upto = jnp.dot(flag, upper, preferred_element_type=F32)
     above = jnp.sum(jnp.dot(lower, flag, preferred_element_type=F32), axis=1, keepdims=True)
     through = (above + upto[:, LANES - 1 :]).astype(jnp.int32)
-    place = (upto + above).astype(jnp.int32) - 1
+    place_ref[...] = jnp.where(mine, (upto + above).astype(jnp.int32) - 1, -1)
     above = above.astype(jnp.int32)
     count = jnp.sum(flag.astype(F32)).astype(jnp.int32)
     lane = iota((rows, LANES), 1)
@@ -175,6 +174,17 @@
     third_stage(2 * pairs - 1, second_b)
     third_stage(2 * pairs, second_a)
 
+
+def weigh_kernel(scen_size, span, total, *refs):
+    value_ref, weighted_ref, place_ref, *rank_refs, send_ref = refs
+    rows = place_ref.shape[0]
+    tile_rows = value_ref.shape[1]
+    scenarios = tile_rows // SLOTS
+    cuts = rows // SLOTS
+    z = lax.axis_index("scen")
+    place = place_ref[...]
+    mine = place >= 0
+    count = jnp.sum(jnp.where(mine, 1.0, 0.0)).astype(jnp.int32)
     ranks = jnp.concatenate([ref[...] for ref in rank_refs] * SLOTS, axis=1).astype(F32)
     weight_sum = jnp.sum(jnp.exp(-iota((8, total), 1).astype(F32) / span), axis=1, keepdims=True)[0:1]
     weight = pltpu.roll(jnp.exp(-ranks / span) / weight_sum, z * rank_refs[0].shape[1], 1)
@@ -263,24 +273,34 @@
         trade_block.reshape(rows, LANES), position.reshape(rows, LANES), *sources, w_in, trade_embed,
         b_mid.reshape(1, hidden), w_mid, w_out,
     )
-    send = pl.pallas_call(
-        functools.partial(price_kernel, fused, scen_size, local_count, total // 20, total),
-        out_shape=pltpu.VMEM((peers, rows + 8, LANES), BF),
-        in_specs=[vmem] * scen_size + [hbm] * len(inputs),
-        out_specs=vmem,
+    value, weighted, place = pl.pallas_call(
+        functools.partial(price_kernel, fused, scen_size, local_count),
+        out_shape=(
+            pltpu.VMEM((tiles, SLOTS * scenarios), F32),
+            pltpu.VMEM((rows, LANES), F32),
+            pltpu.VMEM((rows, LANES), jnp.int32),
+        ),
+        in_specs=[hbm] * len(inputs),
+        out_specs=(vmem, vmem, vmem),
         scratch_shapes=[
             *(pltpu.VMEM(x.shape, x.dtype) for x in inputs),
             pltpu.VMEM((local_count * trade_size, scenarios, hidden), F32),
             pltpu.VMEM((trades, hidden), F32),
             pltpu.VMEM((rows + 8, LANES), jnp.int32),
             pltpu.SMEM((rows + 8, LANES), jnp.int32),
-            pltpu.VMEM((rows, LANES), F32),
-            pltpu.VMEM((tiles, SLOTS * scenarios), F32),
             *(pltpu.VMEM((step_rows, hidden), BF) for _ in range(4)),
             pltpu.SemaphoreType.DMA((len(inputs) + 1,)),
         ],
+        cost_estimate=pl.CostEstimate(flops=10**10, transcendentals=0, bytes_accessed=2 * 10**6),
         name="price",
-    )(*(held(rank) for rank in ranks), *inputs)
+    )(*inputs)
+    send = pl.pallas_call(
+        functools.partial(weigh_kernel, scen_size, total // 20, total),
+        out_shape=pltpu.VMEM((peers, rows + 8, LANES), BF),
+        in_specs=[vmem] * (3 + scen_size),
+        out_specs=vmem,
+        name="weigh",
+    )(held(value), held(weighted), held(place), *(held(rank) for rank in ranks))
     got = lax.all_to_all(send, ("mkt", "scen"), split_axis=0, concat_axis=0, tiled=True)
     book_pnl, marginal, shortfall = pl.pallas_call(
         functools.partial(total_kernel, scen_size, quarter),

time: 41.5 us -> 37 us (0.89)
  blocking collectives: 14.5 us -> 12 us
  waiting for transfers between devices: 2.22 us -> 0.01 us
    all_to_all x1, blocking collectives: 14.5 us -> 12 us  [local(): lax.all_to_all(send, ('mkt', 'scen'), split_axis=0, concat_axis=0, tiled=...]
    ppermute x3, waiting for transfers between devices: 2.22 us -> 0.01 us  [local(): lax.ppermute(rank_row, 'scen', [(i, (i + k) % scen_size) for i in range(s...]
    pallas_call x0 -> x1, Pallas kernels: none -> 0.84 us  [local(): pl.pallas_call(functools.partial(weigh_kernel, scen_size, total // 20, to...]
    pallas_call x1, Pallas kernels: 15.6 us -> 15 us  [local(): pl.pallas_call(functools.partial(price_kernel, fused, scen_size, local_co...]
  transfers between devices with their start and end apart: 3 -> 3, of which waited for: 2 -> 0; matrix products, arithmetic and copies ran while one was open for 0% -> 0% of each run, Pallas kernels for 0% -> 41%
where the time goes in v4:
time: 37 us; the launch traced here: 36.8 us
  Pallas kernels  16.4 us (44%)
  blocking collectives  12 us (32%)
  starting transfers between devices  6.99 us (19%)
  between operations  0.68 us (2%)
  local copies, waits for them, and re-layouts  0.65 us (2%)
    pallas_call x1, Pallas kernels, local(): pl.pallas_call(functools.partial(price_kernel, fused, scen_size, local_co...  15 us
    all_to_all x1, blocking collectives, local(): lax.all_to_all(send, ('mkt', 'scen'), split_axis=0, concat_axis=0, tiled=...  12 us
    ppermute x3, starting transfers between devices, local(): lax.ppermute(rank_row, 'scen', [(i, (i + k) % scen_size) for i in range(s...  6.99 us
    pallas_call x1, Pallas kernels, local(): pl.pallas_call(functools.partial(weigh_kernel, scen_size, total // 20, to...  0.84 us
  transfers between devices with their start and end apart: 3, of which 0 were waited for; matrix products, arithmetic and copies ran while one was open for 0% of the time, Pallas kernels for 41%

profile of v4, /device:TPU:0, one launch (start us, length us, event | category | flops | bytes accessed | tf_op | source)
XLA Modules:
  0.0 36.8 jit_solution(11494251309138295302)
XLA Ops:
  0.6 0.0 copy-start
  0.6 0.6 %copy-done = s32[16]{0:T(128)S(1)} copy-done((s32[16]{0:T(128)S(1)}, s32[16]{0:T(128)}, u32[]{:S(2)}) %copy-start) | copy-done | bytes 88
  1.3 3.1 %collective-permute-start.2 = (s32[1,16]{1,0:T(1,128)S(1)}, s32[1,16]{1,0:T(1,128)S(1)}, u32[]{:S(2)}, u32[]{:S(2)}) collective-permute-start(s32[1,16]{1,0:T(1,128)S(1)} %bitcast.7), channel_id=1, source_target_pairs={{0,1},{1,2},{2,3},{3,0},{4,5},{5,6},{6,7},{7,4},{8,9},{9,10},{10,1... | collective-permute-start | bytes 200 | tf_op jit(solution)/shard_map/ppermute | solution.py:247
  4.3 2.6 %collective-permute-start.1 = (s32[1,16]{1,0:T(1,128)S(1)}, s32[1,16]{1,0:T(1,128)S(1)}, u32[]{:S(2)}, u32[]{:S(2)}) collective-permute-start(s32[1,16]{1,0:T(1,128)S(1)} %bitcast.8), channel_id=1, source_target_pairs={{0,2},{1,3},{2,0},{3,1},{4,6},{5,7},{6,4},{7,5},{8,10},{9,11},{10,... | collective-permute-start | bytes 200 | tf_op jit(solution)/shard_map/ppermute | solution.py:247
  6.9 1.3 %collective-permute-start = (s32[1,16]{1,0:T(1,128)S(1)}, s32[1,16]{1,0:T(1,128)S(1)}, u32[]{:S(2)}, u32[]{:S(2)}) collective-permute-start(s32[1,16]{1,0:T(1,128)S(1)} %bitcast.9), channel_id=1, source_target_pairs={{0,3},{1,0},{2,1},{3,2},{4,7},{5,4},{6,5},{7,6},{8,11},{9,8},{10,9... | collective-permute-start | bytes 200 | tf_op jit(solution)/shard_map/ppermute | solution.py:247
  8.3 15.0 %price.1 = (f32[640,256]{1,0:T(8,128)S(1)}, f32[16,128]{1,0:T(8,128)S(1)}, s32[16,128]{1,0:T(8,128)S(1)}) custom-call(s32[16,128]{1,0:T(8,128)} %bitcast.11, f32[16,128]{1,0:T(8,128)} %bitcast.12, bf16[64,512]{1,0:T(8,128)(2,1)} %refs_2_.1, bf16[16,128,128]{2,1,0:T(8,128)(2,1)} %refs_3_.1, bf16[128,256]{1,0:T(8,128)(2,1)} %refs_4_.1, ...), custom_call_target="tpu_custom_call" | custom-call | flops 10000000000 | bytes 2000000 | tf_op jit(solution)/shard_map/price/pallas_call | solution.py:276
  23.3 0.0 collective-permute-done.2.refs_6_
  23.3 0.0 collective-permute-done.1.refs_5_
  23.3 0.0 collective-permute-done.refs_4_
  23.3 0.8 %weigh.1 = bf16[32,24,128]{2,1,0:T(8,128)(2,1)S(1)} custom-call(f32[640,256]{1,0:T(8,128)S(1)} %get-tuple-element.9.refs_0_, f32[16,128]{1,0:T(8,128)S(1)} %get-tuple-element.10.refs_1_, s32[16,128]{1,0:T(8,128)S(1)} %get-tuple-element.11.refs_2_, s32[1,16]{1,0:T(1,128)S(1)} %bitcast.10, s32[1,16]{1,0:T(1,128)S(1)} %collective-permute-done.refs_4_, ...), custom_call_target="tpu_custom_call" | custom-call | tf_op jit(solution)/shard_map/weigh/pallas_call | solution.py:297
  24.1 12.0 %all_to_all.5.got_ref = bf16[32,24,128]{2,1,0:T(8,128)(2,1)S(1)} all-to-all(bf16[32,24,128]{2,1,0:T(8,128)(2,1)S(1)} %weigh.1), channel_id=1, replica_groups=mesh['mkt'=8,'trade'=1,'scen'=4] {'mkt','scen'}, dimensions={0} | all-to-all | bytes 393216 | tf_op jit(solution)/shard_map/all_to_all | solution.py:304
  36.2 0.6 %total.1 = (f32[1,16]{1,0:T(1,128)}, f32[16,128]{1,0:T(8,128)}, f32[1,1]{1,0:T(1,128)}) custom-call(bf16[32,24,128]{2,1,0:T(8,128)(2,1)S(1)} %all_to_all.5.got_ref), custom_call_target="tpu_custom_call" | custom-call | tf_op jit(solution)/shard_map/total/pallas_call | solution.py:305
Async XLA Ops:
  0.6 0.7 %copy-start = (s32[16]{0:T(128)S(1)}, s32[16]{0:T(128)}, u32[]{:S(2)}) copy-start(s32[16]{0:T(128)} %param.15) | copy-start | bytes 196
  1.3 22.0 %collective-permute-start.2 = (s32[1,16]{1,0:T(1,128)S(1)}, s32[1,16]{1,0:T(1,128)S(1)}, u32[]{:S(2)}, u32[]{:S(2)}) collective-permute-start(s32[1,16]{1,0:T(1,128)S(1)} %bitcast.7), channel_id=1, source_target_pairs={{0,1},{1,2},{2,3},{3,0},{4,5},{5,6},{6,7},{7,4},{8,9},{9,10},{10,1... | collective-permute-start | bytes 200 | tf_op jit(solution)/shard_map/ppermute | solution.py:247
  4.3 18.9 %collective-permute-start.1 = (s32[1,16]{1,0:T(1,128)S(1)}, s32[1,16]{1,0:T(1,128)S(1)}, u32[]{:S(2)}, u32[]{:S(2)}) collective-permute-start(s32[1,16]{1,0:T(1,128)S(1)} %bitcast.8), channel_id=1, source_target_pairs={{0,2},{1,3},{2,0},{3,1},{4,6},{5,7},{6,4},{7,5},{8,10},{9,11},{10,... | collective-permute-start | bytes 200 | tf_op jit(solution)/shard_map/ppermute | solution.py:247
  6.9 16.3 %collective-permute-start = (s32[1,16]{1,0:T(1,128)S(1)}, s32[1,16]{1,0:T(1,128)S(1)}, u32[]{:S(2)}, u32[]{:S(2)}) collective-permute-start(s32[1,16]{1,0:T(1,128)S(1)} %bitcast.9), channel_id=1, source_target_pairs={{0,3},{1,0},{2,1},{3,2},{4,7},{5,4},{6,5},{7,6},{8,11},{9,8},{10,9... | collective-permute-start | bytes 200 | tf_op jit(solution)/shard_map/ppermute | solution.py:247
